TPU v7x, 32 devices: a whole 2x2x4 slice. The times are simulated.
32 devices in a mesh: shard: 4 (over y, x), context: 4 (over z), tensor: 2 (over core).
Axes of the slice: x: 2, y: 2, z: 4, core: 2. Of those that a mesh axis runs over, the one named last changes fastest.
Arguments:
- hidden_in: bfloat16 [8, 1024, 2048], P('shard', 'context'), may hold values from -6 to 6
- cotangent: bfloat16 [8, 1024, 2048], P('shard', 'context'), may hold values from -6 to 6
- seq_lengths: int32 [8], P('shard'), may hold values from 256 to 1024, as said below
- adapter_ids: int32 [8], P('shard'), may hold values from 0 to 7
- attn_gain: bfloat16 [2048], replicated, may hold values from 0.25 to 1.75
- ffn_gain: bfloat16 [2048], replicated, may hold values from 0.25 to 1.75
- query_weight: bfloat16 [2048, 2048], P(('shard', 'context'), 'tensor'), may hold values from -0.125 to 0.125
- key_weight: bfloat16 [2048, 1024], P(('shard', 'context'), 'tensor'), may hold values from -0.125 to 0.125
- value_weight: bfloat16 [2048, 1024], P(('shard', 'context'), 'tensor'), may hold values from -0.125 to 0.125
- output_weight: bfloat16 [2048, 2048], P(('shard', 'context'), 'tensor'), may hold values from -0.5 to 0.5
- gate_weight: bfloat16 [2048, 8192], P(('shard', 'context'), 'tensor'), may hold values from -0.125 to 0.125
- up_weight: bfloat16 [2048, 8192], P(('shard', 'context'), 'tensor'), may hold values from -0.125 to 0.125
- down_weight: bfloat16 [2048, 8192], P(('shard', 'context'), 'tensor'), may hold values from -0.0625 to 0.0625
- qkv_entry: bfloat16 [2048, 128], P(('shard', 'context')), may hold values from -0.125 to 0.125
- query_exit: bfloat16 [128, 2048], P(('shard', 'context'), 'tensor'), may hold values from -1.5 to 1.5
- key_exit: bfloat16 [128, 1024], P(('shard', 'context'), 'tensor'), may hold values from -1.5 to 1.5
- value_exit: bfloat16 [128, 1024], P(('shard', 'context'), 'tensor'), may hold values from -1.5 to 1.5
- attn_entry: bfloat16 [128, 2048], P(('shard', 'context'), 'tensor'), may hold values from -0.5 to 0.5
- attn_exit: bfloat16 [2048, 128], P(('shard', 'context')), may hold values from -1.5 to 1.5
- gate_entry: bfloat16 [2048, 128], P(('shard', 'context')), may hold values from -0.125 to 0.125
- gate_exit: bfloat16 [128, 8192], P(('shard', 'context'), 'tensor'), may hold values from -1.5 to 1.5
- up_entry: bfloat16 [2048, 128], P(('shard', 'context')), may hold values from -0.125 to 0.125
- up_exit: bfloat16 [128, 8192], P(('shard', 'context'), 'tensor'), may hold values from -1.5 to 1.5
- down_entry: bfloat16 [128, 8192], P(('shard', 'context'), 'tensor'), may hold values from -0.0625 to 0.0625
- down_exit: bfloat16 [2048, 128], P(('shard', 'context')), may hold values from -1.5 to 1.5
Outputs:
- layer_out: bfloat16 [8, 1024, 2048], P('shard', 'context')
- input_grad: bfloat16 [8, 1024, 2048], P('shard', 'context')
- qkv_entry_grad: float32 [2048, 128], P(('shard', 'context'))
- query_exit_grad: float32 [128, 2048], P(('shard', 'context'), 'tensor')
- key_exit_grad: float32 [128, 1024], P(('shard', 'context'), 'tensor')
- value_exit_grad: float32 [128, 1024], P(('shard', 'context'), 'tensor')
- attn_entry_grad: float32 [128, 2048], P(('shard', 'context'), 'tensor')
- attn_exit_grad: float32 [2048, 128], P(('shard', 'context'))
- gate_entry_grad: float32 [2048, 128], P(('shard', 'context'))
- gate_exit_grad: float32 [128, 8192], P(('shard', 'context'), 'tensor')
- up_entry_grad: float32 [2048, 128], P(('shard', 'context'))
- up_exit_grad: float32 [128, 8192], P(('shard', 'context'), 'tensor')
- down_entry_grad: float32 [128, 8192], P(('shard', 'context'), 'tensor')
- down_exit_grad: float32 [2048, 128], P(('shard', 'context'))
Inputs may be any that keep to these rules, and one draw needn't show every extreme that they name: Each sequence's valid positions are the first seq_lengths of its slot; in every draw some sequence fills its whole slot of 1024 and some has exactly 256.
All inputs are finite; a program needn't handle non-finite values.
Results may differ from a plain program's by a relative error of at most 0.019.
Values may be sent and summed in bfloat16 or wider, within the bound.
A program may use at most 320 MiB of HBM per device.

v0:
```python
import math

import jax
import jax.numpy as jnp
from jax import lax
from jax.sharding import PartitionSpec as P

HD = 128
RANK = 16
EPSILON = 1e-05
ROPE_BASE = 1000000.0
MASKED = -1e30
F32 = jnp.float32
BF16 = jnp.bfloat16
PLANE = ("tensor", "shard")


def dot(left, right):
    return jnp.dot(left, right, preferred_element_type=F32)


def dot_t(left, right):
    return lax.dot_general(left, right, (((1,), (1,)), ((), ())), preferred_element_type=F32)


def token_sum(left, right):
    return lax.dot_general(left, right, (((0,), (0,)), ((), ())), preferred_element_type=F32)


def rms_scale(values, gain):
    return values * lax.rsqrt(jnp.mean(values * values, axis=-1, keepdims=True) + EPSILON) * gain


def norm_back(values, gain, grad):
    r = lax.rsqrt(jnp.mean(values * values, axis=-1, keepdims=True) + EPSILON)
    scaled = grad * gain
    return r * scaled - values * (r * r * r * jnp.mean(values * scaled, axis=-1, keepdims=True))


def rope_tables(length):
    half = HD // 2
    inverse = ROPE_BASE ** (-2.0 * jnp.arange(half).astype(F32) / HD)
    angles = jnp.arange(length).astype(F32)[:, None] * inverse[None, :]
    return jnp.cos(angles), jnp.sin(angles)


def rotate(values, cosine, sine):
    half = HD // 2
    first, second = values[..., :half], values[..., half:]
    return jnp.concatenate(
        [first * cosine - second * sine, second * cosine + first * sine], axis=-1
    )


def gather_tokens(values):
    return lax.all_gather(values, PLANE, axis=0, tiled=True)


def scatter_tokens(values):
    return lax.psum_scatter(
        values.astype(BF16), PLANE, scatter_dimension=0, tiled=True
    ).astype(F32)


def shards(
    hidden_in,
    cotangent,
    seq_lengths,
    adapter_ids,
    attn_gain,
    ffn_gain,
    query_weight,
    key_weight,
    value_weight,
    output_weight,
    gate_weight,
    up_weight,
    down_weight,
    qkv_entry,
    query_exit,
    key_exit,
    value_exit,
    attn_entry,
    attn_exit,
    gate_entry,
    gate_exit,
    up_entry,
    up_exit,
    down_entry,
    down_exit,
):
    n_s, n_c = lax.axis_size("shard"), lax.axis_size("context")
    s, t = lax.axis_index("shard"), lax.axis_index("tensor")
    groups, local_len, width = hidden_in.shape
    block = width // (n_s * n_c)
    full_len = local_len * n_c
    tokens = groups * full_len
    ranks = qkv_entry.shape[1]
    swap = [(a * n_c + b, b * n_c + a) for a in range(n_s) for b in range(n_c)]

    def to_layer(values):
        own = lax.dynamic_index_in_dim(values, t, 0, keepdims=False)
        own = own.reshape(local_len, n_s, n_c, block).transpose(0, 2, 1, 3)
        return lax.ppermute(own.reshape(local_len, width), ("shard", "context"), swap)

    def from_layer(values):
        own = values.reshape(local_len, n_c, n_s, block).transpose(0, 2, 1, 3)
        own = lax.ppermute(own.reshape(local_len, width), ("shard", "context"), swap)
        return lax.all_gather(own, "tensor", axis=0)

    def features(vector):
        return vector.reshape(n_s, n_c, block).transpose(1, 0, 2).reshape(width).astype(F32)

    def split(weights):
        rows, cols = weights.shape
        return weights.reshape(rows, n_s, cols // n_s).transpose(1, 0, 2)

    kv_heads_here = key_weight.shape[1] // HD
    kv_take = max(1, kv_heads_here // n_s)
    kv_first = [q * kv_heads_here // n_s for q in range(n_s)]

    def split_kv(weights):
        return jnp.stack([weights[:, h * HD : (h + kv_take) * HD] for h in kv_first])

    x_low = to_layer(hidden_in)
    cot_low = to_layer(cotangent)
    lengths, ids = lax.ppermute(
        jnp.stack([seq_lengths, adapter_ids]), ("shard", "context"), swap
    )
    gain_one, gain_two = features(attn_gain), features(ffn_gain)
    positions = s * local_len + jnp.arange(local_len)
    valid = (positions < lengths[t]).astype(F32)[:, None]
    chosen = (jnp.arange(ranks)[None, :] // RANK == ids[:, None]).astype(F32)
    select_own = chosen[t][None, :]
    select_all = jnp.broadcast_to(chosen[:, None, :], (groups, full_len, ranks)).reshape(
        tokens, ranks
    )

    def spread(pieces):
        swapped = lax.all_to_all(pieces, "shard", 0, 0, tiled=True)
        return lax.all_gather(swapped, "context", axis=0)

    attn_w = spread(
        jnp.concatenate(
            [split(query_weight), split_kv(key_weight), split_kv(value_weight), split(output_weight)],
            axis=2,
        )
    ).reshape(width, -1)
    attn_e = (
        spread(
            jnp.concatenate(
                [split(query_exit), split_kv(key_exit), split_kv(value_exit), split(attn_entry)],
                axis=2,
            )
        )
        .transpose(1, 0, 2, 3)
        .reshape(ranks, -1)
    )
    ffn_w = spread(
        jnp.concatenate([split(gate_weight), split(up_weight), split(down_weight)], axis=2)
    ).reshape(width, -1)
    ffn_e = (
        spread(jnp.concatenate([split(gate_exit), split(up_exit), split(down_entry)], axis=2))
        .transpose(1, 0, 2, 3)
        .reshape(ranks, -1)
    )
    entries = lax.all_gather(
        jnp.concatenate([qkv_entry, attn_exit, gate_entry, up_entry, down_exit], axis=1),
        ("context", "shard"),
        axis=0,
        tiled=True,
    )
    qkv_in, attn_out, gate_in, up_in, down_out = (
        entries[:, i * ranks : (i + 1) * ranks] for i in range(5)
    )
    q_cols = query_weight.shape[1] // n_s
    k_cols = kv_take * HD
    f_cols = gate_weight.shape[1] // n_s
    w_qkv, w_o = attn_w[:, : q_cols + 2 * k_cols], attn_w[:, q_cols + 2 * k_cols :]
    e_qkv, e_o = attn_e[:, : q_cols + 2 * k_cols], attn_e[:, q_cols + 2 * k_cols :]
    w_g, w_u, w_d = (ffn_w[:, i * f_cols : (i + 1) * f_cols] for i in range(3))
    e_g, e_u, e_d = (ffn_e[:, i * f_cols : (i + 1) * f_cols] for i in range(3))

    inputs = x_low.astype(F32)
    n1 = gather_tokens(rms_scale(inputs, gain_one).astype(BF16))
    en_qkv = (select_all * dot(n1, qkv_in)).astype(BF16)
    qkv = dot(n1, w_qkv) + dot(en_qkv, e_qkv)
    heads = q_cols // HD
    repeat = heads // kv_take
    cosine, sine = rope_tables(full_len)
    cos_h, sin_h = cosine[None, :, None, :], sine[None, :, None, :]
    query = rotate(qkv[:, :q_cols].reshape(groups, full_len, heads, HD), cos_h, sin_h)
    query = query.astype(BF16).reshape(groups, full_len, kv_take, repeat, HD)
    key = rotate(
        qkv[:, q_cols : q_cols + k_cols].reshape(groups, full_len, kv_take, HD), cos_h, sin_h
    ).astype(BF16)
    value = qkv[:, q_cols + k_cols :].astype(BF16).reshape(groups, full_len, kv_take, HD)
    scale = 1.0 / math.sqrt(HD)
    at = jnp.arange(full_len)
    allowed = (at[None, None, :] <= at[None, :, None]) & (at[None, None, :] < lengths[:, None, None])
    allowed = allowed[:, None, None]
    scores = jnp.einsum("gqcrd,gkcd->gcrqk", query, key, preferred_element_type=F32) * scale
    scores = jnp.where(allowed, scores, MASKED)
    largest = jnp.max(scores, axis=-1, keepdims=True)
    exponent = jnp.exp(scores - largest)
    totals = jnp.sum(exponent, axis=-1, keepdims=True)
    probs = exponent / totals
    attended = jnp.einsum(
        "gcrqk,gkcd->gqcrd", probs.astype(BF16), value, preferred_element_type=F32
    )
    att = attended.reshape(tokens, q_cols).astype(BF16)
    total = scatter_tokens(jnp.concatenate([dot_t(att, w_o), dot_t(att, e_o)], axis=1))
    en_attn = (select_own * total[:, width:]).astype(BF16)
    mid = inputs + total[:, :width] + dot_t(en_attn, attn_out)

    n2_own = rms_scale(mid, gain_two).astype(BF16)
    both = gather_tokens(jnp.concatenate([n2_own, en_attn], axis=1))
    n2, en_attn_all = both[:, :width], both[:, width:]
    en_gate = (select_all * dot(n2, gate_in)).astype(BF16)
    en_up = (select_all * dot(n2, up_in)).astype(BF16)
    gate = dot(n2, w_g) + dot(en_gate, e_g)
    up = dot(n2, w_u) + dot(en_up, e_u)
    sig = jax.nn.sigmoid(gate)
    hidden = (gate * sig * up).astype(BF16)
    total = scatter_tokens(jnp.concatenate([dot_t(hidden, w_d), dot_t(hidden, e_d)], axis=1))
    en_down = (select_own * total[:, width:]).astype(BF16)
    layer_sum = mid + total[:, :width] + dot_t(en_down, down_out)
    layer_out = from_layer((valid * layer_sum).astype(BF16))

    grad_out = valid * cot_low.astype(F32)
    g_low = gather_tokens(grad_out.astype(BF16))
    g_en_down = (select_all * dot(g_low, down_out)).astype(BF16)
    down_entry_grad = token_sum(g_en_down, hidden)
    g_hidden = dot(g_low, w_d) + dot(g_en_down, e_d)
    g_gate = (g_hidden * up * (sig * (1.0 + gate * (1.0 - sig)))).astype(BF16)
    g_up = (g_hidden * gate * sig).astype(BF16)
    gate_exit_grad = token_sum(en_gate, g_gate)
    up_exit_grad = token_sum(en_up, g_up)
    total = scatter_tokens(
        jnp.concatenate(
            [dot_t(g_gate, w_g) + dot_t(g_up, w_u), dot_t(g_gate, e_g), dot_t(g_up, e_u)], axis=1
        )
    )
    g_en_gate = (select_own * total[:, width : width + ranks]).astype(BF16)
    g_en_up = (select_own * total[:, width + ranks :]).astype(BF16)
    g_two = total[:, :width] + dot_t(g_en_gate, gate_in) + dot_t(g_en_up, up_in)
    g_mid = grad_out + norm_back(mid, gain_two, g_two)
    both = gather_tokens(
        jnp.concatenate([g_mid.astype(BF16), g_en_gate, g_en_up, en_down], axis=1)
    )
    g_mid_all = both[:, :width]
    g_en_gate_all, g_en_up_all, en_down_all = (
        both[:, width + i * ranks : width + (i + 1) * ranks] for i in range(3)
    )

    def rows_of(values):
        mine = lax.dynamic_index_in_dim(
            values.reshape(tokens, n_c, n_s, block), s, 2, keepdims=False
        )
        return mine.reshape(tokens, n_c * block)

    n2_rows = rows_of(n2)
    gate_entry_grad = token_sum(n2_rows, g_en_gate_all)
    up_entry_grad = token_sum(n2_rows, g_en_up_all)
    down_exit_grad = token_sum(rows_of(g_low), en_down_all)
    attn_exit_grad = token_sum(rows_of(g_mid_all), en_attn_all)

    g_en_attn = (select_all * dot(g_mid_all, attn_out)).astype(BF16)
    attn_entry_grad = token_sum(g_en_attn, att)
    g_att = (dot(g_mid_all, w_o) + dot(g_en_attn, e_o)).astype(BF16)
    g_heads = g_att.reshape(groups, full_len, kv_take, repeat, HD)
    g_probs = jnp.einsum("gqcrd,gkcd->gcrqk", g_heads, value, preferred_element_type=F32)
    centre = jnp.sum(probs * g_probs, axis=-1, keepdims=True)
    g_scores = (probs * (g_probs - centre)).astype(BF16)
    g_query = jnp.einsum("gcrqk,gkcd->gqcrd", g_scores, key, preferred_element_type=F32) * scale
    g_key = jnp.einsum("gcrqk,gqcrd->gkcd", g_scores, query, preferred_element_type=F32) * scale
    g_value = jnp.einsum(
        "gcrqk,gqcrd->gkcd", probs.astype(BF16), g_heads, preferred_element_type=F32
    )
    g_qkv = jnp.concatenate(
        [
            rotate(g_query.reshape(groups, full_len, heads, HD), cos_h, -sin_h).reshape(tokens, -1),
            rotate(g_key, cos_h, -sin_h).reshape(tokens, -1),
            g_value.reshape(tokens, -1),
        ],
        axis=1,
    ).astype(BF16)
    qkv_exit_grad = token_sum(en_qkv, g_qkv)
    total = scatter_tokens(jnp.concatenate([dot_t(g_qkv, w_qkv), dot_t(g_qkv, e_qkv)], axis=1))
    g_en_qkv = (select_own * total[:, width:]).astype(BF16)
    g_one = total[:, :width] + dot_t(g_en_qkv, qkv_in)
    input_grad = from_layer((g_mid + norm_back(inputs, gain_one, g_one)).astype(BF16))
    qkv_entry_grad = token_sum(rows_of(n1), gather_tokens(g_en_qkv))

    exits = jnp.concatenate(
        [qkv_exit_grad, attn_entry_grad, gate_exit_grad, up_exit_grad, down_entry_grad], axis=1
    )
    cols = exits.shape[1]
    per = ranks // (n_s * n_c)
    exits = lax.psum_scatter(
        exits.reshape(n_s, n_c, per, cols).transpose(1, 0, 2, 3), "context", scatter_dimension=0
    )
    exits = lax.all_to_all(exits, "shard", 0, 0, tiled=True)

    def join(first, count):
        part = exits[:, :, first : first + count]
        return part.transpose(1, 0, 2).reshape(per, n_s * count)

    def join_kv(first):
        part = exits[:, :, first : first + k_cols]
        copies = n_s * kv_take // kv_heads_here
        part = part.reshape(n_s // copies, copies, per, k_cols).sum(axis=1)
        return part.transpose(1, 0, 2).reshape(per, kv_heads_here * HD)

    a = q_cols + 2 * k_cols
    f = a + q_cols
    rows = lax.psum_scatter(
        jnp.concatenate(
            [qkv_entry_grad, attn_exit_grad, gate_entry_grad, up_entry_grad, down_exit_grad], axis=1
        ).reshape(n_c, block, 5 * ranks),
        "context",
        scatter_dimension=0,
    )
    qkv_eg, attn_xg, gate_eg, up_eg, down_xg = (
        rows[:, i * ranks : (i + 1) * ranks] for i in range(5)
    )
    return (
        layer_out,
        input_grad,
        qkv_eg,
        join(0, q_cols),
        join_kv(q_cols),
        join_kv(q_cols + k_cols),
        join(a, q_cols),
        attn_xg,
        gate_eg,
        join(f, f_cols),
        up_eg,
        join(f + f_cols, f_cols),
        join(f + 2 * f_cols, f_cols),
        down_xg,
    )


def solution(mesh):
    in_specs = (
        P("shard", "context", None),
        P("shard", "context", None),
        P("shard"),
        P("shard"),
        P(),
        P(),
        P(("shard", "context"), "tensor"),
        P(("shard", "context"), "tensor"),
        P(("shard", "context"), "tensor"),
        P(("shard", "context"), "tensor"),
        P(("shard", "context"), "tensor"),
        P(("shard", "context"), "tensor"),
        P(("shard", "context"), "tensor"),
        P(("shard", "context"), None),
        P(("shard", "context"), "tensor"),
        P(("shard", "context"), "tensor"),
        P(("shard", "context"), "tensor"),
        P(("shard", "context"), "tensor"),
        P(("shard", "context"), None),
        P(("shard", "context"), None),
        P(("shard", "context"), "tensor"),
        P(("shard", "context"), None),
        P(("shard", "context"), "tensor"),
        P(("shard", "context"), "tensor"),
        P(("shard", "context"), None),
    )
    out_specs = (
        P("shard", "context", None),
        P("shard", "context", None),
        P(("shard", "context"), None),
        P(("shard", "context"), "tensor"),
        P(("shard", "context"), "tensor"),
        P(("shard", "context"), "tensor"),
        P(("shard", "context"), "tensor"),
        P(("shard", "context"), None),
        P(("shard", "context"), None),
        P(("shard", "context"), "tensor"),
        P(("shard", "context"), None),
        P(("shard", "context"), "tensor"),
        P(("shard", "context"), "tensor"),
        P(("shard", "context"), None),
    )
    return jax.shard_map(shards, mesh=mesh, in_specs=in_specs, out_specs=out_specs, check_vma=False)
```

profile of v0, /device:TPU:0, one launch (start us, length us, event | category | flops | bytes accessed | tf_op | source)
XLA Modules:
  0.0 1481.1 jit_solution(7762297496031719732)
XLA Ops:
  19.5 102.0 %all_to_all.25 = bf16[4,128,768]{1,2,0:T(8,128)(2,1)S(1)} all-to-all(bf16[4,128,768]{1,2,0:T(8,128)(2,1)S(1)} %pad_maximum_fusion.10), channel_id=1, replica_groups=mesh['shard'=4,'context'=4,'tensor'=2] {'shard'}, dimensions={0} | all-to-all | bytes 1572864 | tf_op jit(solution)/shard_map/all_to_all | solution.py:140
  124.0 8.2 all-to-all-start.1
  132.6 3.2 fusion.98
  137.1 14.0 all-gather.1
  151.1 34.5 %all-gather.16.cloned.1.call-done = bf16[2048,2048]{0,1:T(8,128)(2,1)} async-done(((bf16[256,2048]{0,1:T(8,128)(2,1)}), bf16[2048,2048]{0,1:T(8,128)(2,1)}) %all-gather.16.cloned.1.call-update) | async-done | bytes 8388624 | tf_op jit(solution)/shard_map/all_gather | solution.py:56
  185.6 5.8 fusion.24
  194.9 56.3 %all-gather.26.cloned.1.call-done = bf16[16,128,768]{2,1,0:T(8,128)(2,1)} async-done(((bf16[4,128,768]{2,1,0:T(8,128)(2,1)}), bf16[16,128,768]{2,1,0:T(8,128)(2,1)}) %all-gather.26.cloned.1.call-update) | async-done | bytes 3145744 | tf_op jit(solution)/shard_map/all_gather | solution.py:141
  251.2 10.1 convolution_add_fusion.3
  264.9 3.4 reshape.517
  268.4 4.6 fusion.125
  275.1 5.8 fusion.5
  280.9 4.0 fusion.4
  287.0 6.6 fusion.46
  296.6 3.6 convolution_convert_fusion.2
  300.2 4.3 pad_maximum_fusion.1
  312.5 90.8 %reduce-scatter.7.cloned.1.call-done = bf16[256,2176]{0,1:T(8,128)(2,1)} async-done(((bf16[2048,2176]{0,1:T(8,128)(2,1)}), bf16[256,2176]{0,1:T(8,128)(2,1)}) %reduce-scatter.7.cloned.1.call-update) | async-done | bytes 1114128 | tf_op jit(solution)/shard_map/reduce_scatter | solution.py:60
  412.6 54.4 %all_to_all.26 = bf16[4,128,3072]{1,2,0:T(8,128)(2,1)S(1)} all-to-all(bf16[4,128,3072]{1,2,0:T(8,128)(2,1)S(1)} %pad_maximum_fusion.4), channel_id=1, replica_groups=mesh['shard'=4,'context'=4,'tensor'=2] {'shard'}, dimensions={0} | all-to-all | bytes 6291456 | tf_op jit(solution)/shard_map/all_to_all | solution.py:140
  470.7 10.2 all_to_all.27
  480.9 18.4 %all-gather.3 = bf16[16,8,3072]{2,1,0:T(8,128)(2,1)S(1)} all-gather(bf16[4,8,3072]{2,1,0:T(8,128)(2,1)S(1)} %all_to_all.27), channel_id=5, replica_groups=mesh['shard'=4,'context'=4,'tensor'=2] {'context'}, dimensions={0}, use_global_device_ids=true | all-gather | bytes 983040 | tf_op jit(solution)/shard_map/all_gather | solution.py:141
  500.3 6.1 fusion.27
  507.2 5.5 fusion.91
  512.7 37.0 %all-gather.20.cloned.1.call-done = bf16[2048,2176]{0,1:T(8,128)(2,1)} async-done(((bf16[256,2176]{0,1:T(8,128)(2,1)}), bf16[2048,2176]{0,1:T(8,128)(2,1)}) %all-gather.20.cloned.1.call-update) | async-done | bytes 8912912 | tf_op jit(solution)/shard_map/all_gather | solution.py:56
  549.7 6.6 fusion.25
  556.4 213.1 %all-gather.28.cloned.1.call-done = bf16[16,128,3072]{2,1,0:T(8,128)(2,1)} async-done(((bf16[4,128,3072]{2,1,0:T(8,128)(2,1)}), bf16[16,128,3072]{2,1,0:T(8,128)(2,1)}) %all-gather.28.cloned.1.call-update) | async-done | bytes 12582928 | tf_op jit(solution)/shard_map/all_gather | solution.py:141
  769.5 12.9 fusion.19
  782.5 4.6 convolution_add_fusion.1
  789.5 12.6 fusion.15
  802.2 4.5 convolution_add_fusion
  806.7 25.9 %multiply_convert_fusion.1 = (bf16[2048,1024]{1,0:T(8,128)(2,1)}, bf16[2048,1024]{1,0:T(8,128)(2,1)}, bf16[2048,1024]{1,0:T(8,128)(2,1)}) fusion(f32[2048,1024]{1,0:T(8,128)} %convolution_add_fusion.1, f32[2048,1024]{1,0:T(8,128)} %convolution_add_fusion, f32[2048,1024]{1,0:T(8,128)} %fusion.91, bf16[2048,2048]{0,1:T(8,128)(2,1)} %all-gather.22.cloned.1.call-done, ...), kind=kOutput, calls=%fused_computation.21 | convolution fusion | flops 8625586176 | bytes 50331648 | tf_op jit(solution)/shard_map/dot_general | solution.py:19
  832.5 3.8 convolution_convert_fusion.6
  836.4 10.7 convolution_convert_fusion.1
  847.1 4.3 pad_maximum_fusion.2
  851.6 3.8 convolution_convert_fusion.5
  857.9 14.4 fusion.17
  872.3 15.1 %add_convert_fusion = bf16[2048,2048]{0,1:T(8,128)(2,1)S(1)} fusion(f32[2048,2048]{0,1:T(8,128)} %fusion.17, bf16[2048,1024]{1,0:T(8,128)(2,1)} %get-tuple-element.58, bf16[2048,3072]{1,0:T(8,128)(2,1)} %bitcast.412), kind=kOutput, calls=%fused_computation.6 | convolution fusion | flops 8598323200 | bytes 33554432 | tf_op jit(solution)/shard_map/dot_general | solution.py:23
  887.4 13.0 pad_maximum_fusion
  900.4 23.2 %reduce-scatter.9.cloned.1.call-done = bf16[256,2176]{0,1:T(8,128)(2,1)} async-done(((bf16[2048,2176]{0,1:T(8,128)(2,1)}), bf16[256,2176]{0,1:T(8,128)(2,1)}) %reduce-scatter.9.cloned.1.call-update) | async-done | bytes 1114128 | tf_op jit(solution)/shard_map/reduce_scatter | solution.py:60
  926.4 77.3 %reduce-scatter.11.cloned.1.call-done = bf16[256,2304]{0,1:T(8,128)(2,1)} async-done(((bf16[2048,2304]{0,1:T(8,128)(2,1)}), bf16[256,2304]{0,1:T(8,128)(2,1)}) %reduce-scatter.11.cloned.1.call-update) | async-done | bytes 1179664 | tf_op jit(solution)/shard_map/reduce_scatter | solution.py:60
  1012.6 62.5 %all-gather.24.cloned.1.call-done = bf16[2048,2432]{0,1:T(8,128)(2,1)} async-done(((bf16[256,2432]{0,1:T(8,128)(2,1)}), bf16[2048,2432]{0,1:T(8,128)(2,1)}) %all-gather.24.cloned.1.call-update) | async-done | bytes 9961488 | tf_op jit(solution)/shard_map/all_gather | solution.py:56
  1075.2 5.9 fusion.28
  1081.1 6.4 fusion.63
  1091.6 10.3 fusion.57
  1101.8 15.9 %fusion = (f32[2,2,1024]{2,1,0:T(2,128)S(1)}, f32[2,1024,1024,2]{2,1,3,0:T(8,128)}) fusion(f32[2,2,1024]{2,1,0:T(2,128)S(1)} %copy-done.75, f32[2,2,1024]{2,1,0:T(2,128)S(1)} %copy-done.73, f32[2,1024,1024,2]{2,1,3,0:T(8,128)} %copy-done.2, pred[2,1024,1024]{1,2,0:T(8,128)(4,1)S(1)} %copy-done.6, bf16[2,1024,128,1]{2,1,3,0:T(8,128)(2,1)S(1)} %bitcast.372, ...), kind=kOutput, calls=%fused_computation.3 | convolution fusion | flops 1098903552 | bytes 37273600 | tf_op jit(solution)/shard_map/gqcrd,gkcd->gcrqk/dot_general | solution.py:272
  1117.8 13.0 fusion.6
  1130.9 3.4 fusion.53
  1134.3 4.9 multiply_bitcast_fusion
  1141.3 3.1 subtract_convert_fusion
  1149.0 4.8 convolution_convert_fusion
  1153.8 4.5 pad_maximum_fusion.3
  1174.0 3.3 constant_dynamic-slice_fusion
  1177.3 3.2 constant_dynamic-slice_fusion.3
  1180.5 8.4 slice.292
  1188.8 3.2 constant_dynamic-slice_fusion.1
  1193.1 8.7 slice.307
  1201.8 3.2 constant_dynamic-slice_fusion.2
  1205.0 64.6 %reduce-scatter.13.cloned.1.call-done = bf16[256,2176]{0,1:T(8,128)(2,1)} async-done(((bf16[2048,2176]{0,1:T(8,128)(2,1)}), bf16[256,2176]{0,1:T(8,128)(2,1)}) %reduce-scatter.13.cloned.1.call-update) | async-done | bytes 1114128 | tf_op jit(solution)/shard_map/reduce_scatter | solution.py:60
  1271.3 24.8 %all_gather.71 = bf16[2048,128]{0,1:T(8,128)(2,1)S(1)} all-gather(bf16[256,128]{0,1:T(8,128)(2,1)S(1)} %fusion.100), channel_id=1, replica_groups=mesh['shard'=4,'context'=4,'tensor'=2] {'tensor','shard'}, dimensions={0}, use_global_device_ids=true | all-gather | bytes 589824 | tf_op jit(solution)/shard_map/all_gather | solution.py:56
  1317.2 96.2 %all-reduce.3.cloned.1.call-done = f32[4,4,8,3840]{3,2,0,1:T(8,128)} async-done(((f32[4,4,8,3840]{3,2,0,1:T(8,128)}), f32[4,4,8,3840]{3,2,0,1:T(8,128)}) %all-reduce.3.cloned.1.call-update) | async-done | bytes 1966096
  1416.0 9.3 all-to-all-start.4
  1425.3 3.9 copy.207
  1429.2 3.3 all-to-all-done.4
  1434.5 25.1 %reduce-scatter.15.cloned.1.call-done = f32[1,128,640]{2,1,0:T(8,128)} async-done(((f32[4,128,640]{2,1,0:T(8,128)}), f32[1,128,640]{2,1,0:T(8,128)}) %reduce-scatter.15.cloned.1.call-update) | async-done | bytes 327696 | tf_op jit(solution)/shard_map/reduce_scatter | solution.py:317
  1461.3 9.1 all-gather.32.cloned.1.call-done
  1470.4 3.9 copy.211
  (364 shorter events, 125.3 us)
Async XLA Ops:
  7.2 143.9 %all-gather.18.cloned.1.call-start = ((), (), s32[]{:S(2)}) async-start(), calls=%async_computation.11 | async-start | bytes 2785280 | tf_op jit(solution)/shard_map/all_gather | solution.py:167
  11.8 173.9 %all-gather.16.cloned.1.call-start = ((), (), s32[]{:S(2)}) async-start(), calls=%async_computation.10 | async-start | bytes 9437184 | tf_op jit(solution)/shard_map/all_gather | solution.py:56
  15.2 0.9 collective-permute-start.1
  16.1 388.7 %copy-start.3 = (bf16[256,2048]{0,1:T(8,128)(2,1)}, bf16[256,2048]{0,1:T(8,128)(2,1)S(1)}, u32[]{:S(2)}) copy-start(bf16[256,2048]{0,1:T(8,128)(2,1)S(1)} %collective-permute-done.1) | copy-start | bytes 3145732
  17.8 233.4 %all-gather.26.cloned.1.call-start = ((), (), s32[]{:S(2)}) async-start(), calls=%async_computation.20 | async-start | bytes 3932160 | tf_op jit(solution)/shard_map/all_gather | solution.py:141
  19.1 103.5 %copy-start.97 = (s32[2]{0:T(128)S(1)}, s32[2]{0:T(128)}, u32[]{:S(2)}) copy-start(s32[2]{0:T(128)} %param.28) | copy-start | bytes 28
  19.2 103.5 %copy-start.98 = (s32[2]{0:T(128)S(1)}, s32[2]{0:T(128)}, u32[]{:S(2)}) copy-start(s32[2]{0:T(128)} %param.27) | copy-start | bytes 28
  19.2 104.2 %copy-start.91 = (bf16[8,512]{1,0:T(8,128)(2,1)S(1)}, bf16[8,512]{1,0:T(8,128)(2,1)}, u32[]{:S(2)}) copy-start(bf16[8,512]{1,0:T(8,128)(2,1)} %param.41) | copy-start | bytes 24580
  19.2 104.2 %copy-start.92 = (bf16[8,512]{1,0:T(8,128)(2,1)S(1)}, bf16[8,512]{1,0:T(8,128)(2,1)}, u32[]{:S(2)}) copy-start(bf16[8,512]{1,0:T(8,128)(2,1)} %param.40) | copy-start | bytes 24580
  19.2 104.2 %copy-start.83 = (bf16[8,1024]{1,0:T(8,128)(2,1)S(1)}, bf16[8,1024]{1,0:T(8,128)(2,1)}, u32[]{:S(2)}) copy-start(bf16[8,1024]{1,0:T(8,128)(2,1)} %param.42) | copy-start | bytes 49156
  19.2 104.2 %copy-start.84 = (bf16[8,1024]{1,0:T(8,128)(2,1)S(1)}, bf16[8,1024]{1,0:T(8,128)(2,1)}, u32[]{:S(2)}) copy-start(bf16[8,1024]{1,0:T(8,128)(2,1)} %param.39) | copy-start | bytes 49156
  122.7 13.1 collective-permute-start
  124.0 13.1 all-to-all-start.1
  132.2 271.0 %reduce-scatter.7.cloned.1.call-start = ((), (), s32[]{:S(2)}) async-start(), calls=%async_computation.12 | async-start | bytes 10027008 | tf_op jit(solution)/shard_map/reduce_scatter | solution.py:60
  137.0 147.9 %copy-start.5 = (pred[2,1024,1024]{1,2,0:T(8,128)(4,1)}, pred[2,1024,1024]{1,2,0:T(8,128)(4,1)S(1)}, u32[]{:S(2)}) copy-start(pred[2,1024,1024]{1,2,0:T(8,128)(4,1)S(1)} %broadcast_and_fusion) | copy-start | bytes 6291460
  151.1 145.0 %copy-start.56 = (bf16[4,4,8,768]{3,2,1,0:T(8,128)(2,1)}, bf16[4,4,8,768]{3,2,1,0:T(8,128)(2,1)S(1)}, u32[]{:S(2)}) copy-start(bf16[4,4,8,768]{3,2,1,0:T(8,128)(2,1)S(1)} %copy.153) | copy-start | bytes 589828
  268.4 4.7 copy-start.17
  268.4 4.7 copy-start.30
  275.1 5.8 copy-start.38
  275.1 5.8 copy-start.40
  280.9 5.8 copy-start.2
  280.9 6.1 copy-start.72
  280.9 6.1 copy-start.59
  304.6 195.7 %all-gather.22.cloned.1.call-start = ((), (), s32[]{:S(2)}) async-start(), calls=%async_computation.15 | async-start | bytes 9437184 | tf_op jit(solution)/shard_map/all_gather | solution.py:56
  306.7 5.7 copy-start.96
  307.7 3.3 collective-permute-start.3
  311.0 93.7 %copy-start.14 = (bf16[256,2048]{0,1:T(8,128)(2,1)}, bf16[256,2048]{0,1:T(8,128)(2,1)S(1)}, u32[]{:S(2)}) copy-start(bf16[256,2048]{0,1:T(8,128)(2,1)S(1)} %collective-permute-done.3) | copy-start | bytes 3145732
  312.3 237.4 %all-gather.20.cloned.1.call-start = ((), (), s32[]{:S(2)}) async-start(), calls=%async_computation.13 | async-start | bytes 10027008 | tf_op jit(solution)/shard_map/all_gather | solution.py:56
  312.4 94.6 %copy-start.70 = (f32[4,4,128]{2,1,0:T(4,128)}, f32[4,4,128]{2,1,0:T(4,128)S(1)}, u32[]{:S(2)}) copy-start(f32[4,4,128]{2,1,0:T(4,128)S(1)} %copy.160) | copy-start | bytes 24580
  312.4 94.0 %copy-start.93 = (f32[128]{0:T(128)}, f32[128]{0:T(128)S(1)}, u32[]{:S(2)}) copy-start(f32[128]{0:T(128)S(1)} %fusion.113) | copy-start | bytes 1540
  409.2 360.3 %all-gather.28.cloned.1.call-start = ((), (), s32[]{:S(2)}) async-start(), calls=%async_computation.21 | async-start | bytes 15728640 | tf_op jit(solution)/shard_map/all_gather | solution.py:141
  469.7 30.5 %copy-start.13 = (bf16[2048,640]{1,0:T(8,128)(2,1)S(1)}, bf16[2048,640]{1,0:T(8,128)(2,1)}, u32[]{:S(2)}) copy-start(bf16[2048,640]{1,0:T(8,128)(2,1)} %all-gather.18.cloned.1.call-done) | copy-start | bytes 7864324
  469.8 453.9 %reduce-scatter.9.cloned.1.call-start = ((), (), s32[]{:S(2)}) async-start(), calls=%async_computation.14 | async-start | bytes 10027008 | tf_op jit(solution)/shard_map/reduce_scatter | solution.py:60
  549.7 237.4 %slice-start = ((s8[8912896]{0:T(1024)(128)(4,1)}), s8[524288]{0:T(1024)(128)(4,1)S(1)}, s32[]{:S(2)}) async-start(s8[8912896]{0:T(1024)(128)(4,1)} %bitcast.322), calls=%async_computation.25 | async-start | bytes 1048576
  769.5 13.0 copy-start.23
  769.5 13.0 copy-start.42
  769.5 17.6 %slice-start.1 = ((s8[8912896]{0:T(1024)(128)(4,1)}), s8[4194304]{0:T(1024)(128)(4,1)S(1)}, s32[]{:S(2)}) async-start(s8[8912896]{0:T(1024)(128)(4,1)} %bitcast.322), calls=%async_computation.26 | async-start | bytes 8388608
  769.5 17.6 %slice-start.2 = ((s8[8912896]{0:T(1024)(128)(4,1)}), s8[4194304]{0:T(1024)(128)(4,1)S(1)}, s32[]{:S(2)}) async-start(s8[8912896]{0:T(1024)(128)(4,1)} %bitcast.322), calls=%async_computation.27 | async-start | bytes 8388608
  789.5 12.7 copy-start.25
  806.7 25.9 %copy-start.43 = (bf16[4,4,8,3072]{3,2,1,0:T(8,128)(2,1)S(1)}, bf16[4,4,8,3072]{3,2,1,0:T(8,128)(2,1)}, u32[]{:S(2)}) copy-start(bf16[4,4,8,3072]{3,2,1,0:T(8,128)(2,1)} %copy.165) | copy-start | bytes 2359300
  851.4 152.4 %reduce-scatter.11.cloned.1.call-start = ((), (), s32[]{:S(2)}) async-start(), calls=%async_computation.16 | async-start | bytes 10616832 | tf_op jit(solution)/shard_map/reduce_scatter | solution.py:60
  900.4 104.8 %copy-start.94 = (f32[128]{0:T(128)S(1)}, f32[128]{0:T(128)}, u32[]{:S(2)}) copy-start(f32[128]{0:T(128)} %copy-done.93) | copy-start | bytes 1540
  900.4 174.8 %all-gather.24.cloned.1.call-start = ((), (), s32[]{:S(2)}) async-start(), calls=%async_computation.17 | async-start | bytes 11206656 | tf_op jit(solution)/shard_map/all_gather | solution.py:56
  1012.2 257.4 %reduce-scatter.13.cloned.1.call-start = ((), (), s32[]{:S(2)}) async-start(), calls=%async_computation.18 | async-start | bytes 10027008 | tf_op jit(solution)/shard_map/reduce_scatter | solution.py:60
  1081.1 6.5 copy-start.28
  1081.1 6.5 copy-start.57
  1091.6 10.3 copy-start.6
  1091.6 10.3 copy-start.60
  1117.8 13.1 copy-start.39
  1117.8 13.1 copy-start.41
  1134.3 7.0 copy-start.10
  1134.3 7.0 copy-start.27
  1158.4 255.1 %all-reduce.3.cloned.1.call-start = ((), (), s32[]{:S(2)}) async-start(), calls=%async_computation.24 | async-start | bytes 3932160
  1168.2 257.1 %all-gather.30.cloned.1.call-start = ((), (), s32[]{:S(2)}) async-start(), calls=%async_computation.22 | async-start | bytes 3145728 | tf_op jit(solution)/shard_map/all_gather | solution.py:109
  1172.0 20.1 %collective-permute-start.2 = (bf16[256,2048]{0,1:T(8,128)(2,1)}, bf16[256,2048]{0,1:T(8,128)(2,1)S(1)}, u32[]{:S(2)}, u32[]{:S(2)}) collective-permute-start(bf16[256,2048]{0,1:T(8,128)(2,1)} %bitcast.74), channel_id=1, source_target_pairs={{0,0},{2,8},{4,16},{6,24},{8,2},{10,10},{12,18},{14,26},{16,4},{18... | collective-permute-start | bytes 3145736 | tf_op jit(solution)/shard_map/ppermute | solution.py:108
  1193.0 266.6 %reduce-scatter.15.cloned.1.call-start = ((), (), s32[]{:S(2)}) async-start(), calls=%async_computation.19 | async-start | bytes 1638400 | tf_op jit(solution)/shard_map/reduce_scatter | solution.py:317
  1269.6 26.5 %copy-start.20 = (bf16[2048,4,1,128]{0,3,2,1:T(8,128)(2,1)S(1)}, bf16[2048,4,1,128]{0,3,2,1:T(8,128)(2,1)}, u32[]{:S(2)}) copy-start(bf16[2048,4,1,128]{0,3,2,1:T(8,128)(2,1)} %constant_dynamic-slice_fusion.3) | copy-start | bytes 6291460
  1269.6 28.0 %copy-start.47 = (bf16[2048,4,1,128]{0,3,2,1:T(8,128)(2,1)S(1)}, bf16[2048,4,1,128]{0,3,2,1:T(8,128)(2,1)}, u32[]{:S(2)}) copy-start(bf16[2048,4,1,128]{0,3,2,1:T(8,128)(2,1)} %constant_dynamic-slice_fusion.2) | copy-start | bytes 6291460
  1271.2 29.1 %copy-start.19 = (f32[256,2176]{0,1:T(8,128)}, f32[256,2176]{0,1:T(8,128)S(1)}, u32[]{:S(2)}) copy-start(f32[256,2176]{0,1:T(8,128)S(1)} %convert_element_type.273) | copy-start | bytes 6684676
  1305.6 5.6 copy-start.4
  1305.6 5.6 copy-start.69
  1311.1 159.3 %all-gather.32.cloned.1.call-start = ((), (), s32[]{:S(2)}) async-start(), calls=%async_computation.23 | async-start | bytes 3145728 | tf_op jit(solution)/shard_map/all_gather | solution.py:109
  1314.9 0.7 collective-permute-start.4
  1416.0 16.5 %all-to-all-start.4 = ((f32[4,8,3840]{2,1,0:T(8,128)}), f32[4,8,3840]{2,1,0:T(8,128)S(1)}, u32[]{:S(2)}, u32[]{:S(2)}) async-start(f32[4,8,3840]{2,1,0:T(8,128)} %dynamic-slice_bitcast_fusion), calls=%async_computation.9 | async-start | bytes 983040 | tf_op jit(solution)/shard_map/all_to_all | solution.py:303
  (61 other events, 137.9 us)
Sparse Core Ops, SparseCore 0:
  11.9 116.4 all-gather.17
  130.8 54.7 all-gather.15
  187.8 63.4 all-gather.25
  304.7 98.5 reduce-scatter.6
  405.0 84.1 all-gather.21
  491.5 58.1 all-gather.19
  551.3 218.1 all-gather.27
  851.5 72.0 reduce-scatter.8
  927.1 76.5 reduce-scatter.10
  1012.3 62.8 all-gather.23
  1158.5 111.0 reduce-scatter.12
  1271.8 141.5 all-reduce.2
  1415.0 9.8 all-gather.29
  1427.0 32.5 reduce-scatter.14
  1461.6 8.7 all-gather.31
where the time goes:
time: 1490 us; the launch traced here: 1480 us
  waiting for transfers between devices  793 us (53%)
  matrix products  246 us (17%)
  blocking collectives  224 us (15%)
  local copies, waits for them, and re-layouts  106 us (7%)
  other arithmetic  71.3 us (5%)
  starting transfers between devices  24.9 us (2%)
  between operations  16 us (1%)
    all_gather x2, waiting for transfers between devices, spread(): return lax.all_gather(swapped, 'context', axis=0)  269 us
    reduce_scatter x4, waiting for transfers between devices, scatter_tokens(): lax.psum_scatter(values.astype(BF16), PLANE, scatter_dimension=0, tiled=T...  256 us
    all_to_all x3, blocking collectives, spread(): swapped = lax.all_to_all(pieces, 'shard', 0, 0, tiled=True)  167 us
    all_gather x4, waiting for transfers between devices, gather_tokens(): return lax.all_gather(values, PLANE, axis=0, tiled=True)  134 us
    dot_general x15, matrix products, dot(): return jnp.dot(left, right, preferred_element_type=F32)  113 us
    unnamed x16, waiting for transfers between devices  96.5 us
    dot_general x15, matrix products, dot_t(): lax.dot_general(left, right, (((1,), (1,)), ((), ())), preferred_element_...  69.2 us
    unnamed x229, local copies, waits for them, and re-layouts  34.9 us
  transfers between devices with their start and end apart: 22, of which 13 were waited for; matrix products, arithmetic and copies ran while one was open for 12% of the time, Pallas kernels for 0%

commit v1 on v0

v1 whole, which is shorter than its diff:
```python
import functools
import math

import jax
import jax.numpy as jnp
from jax import lax
from jax.experimental import pallas as pl
from jax.experimental.pallas import tpu as pltpu
from jax.sharding import PartitionSpec as P

HD = 128
RANK = 16
EPSILON = 1e-05
ROPE_BASE = 1000000.0
MASKED = -1e30
F32 = jnp.float32
BF16 = jnp.bfloat16
MESH = pl.DeviceIdType.MESH


def dot(left, right):
    return jnp.dot(left, right, preferred_element_type=F32)


def dot_t(left, right):
    return lax.dot_general(left, right, (((1,), (1,)), ((), ())), preferred_element_type=F32)


def token_sum(left, right):
    return lax.dot_general(left, right, (((0,), (0,)), ((), ())), preferred_element_type=F32)


def rms_scale(values, gain):
    return values * lax.rsqrt(jnp.mean(values * values, axis=-1, keepdims=True) + EPSILON) * gain


def norm_back(values, gain, grad):
    r = lax.rsqrt(jnp.mean(values * values, axis=-1, keepdims=True) + EPSILON)
    scaled = grad * gain
    return r * scaled - values * (r * r * r * jnp.mean(values * scaled, axis=-1, keepdims=True))


def rope(values, cosine, sine):
    return values * cosine + pltpu.roll(values, HD // 2, 1) * sine


def head_tables(positions):
    half = HD // 2
    inverse = ROPE_BASE ** (-2.0 * jnp.arange(half).astype(F32) / HD)
    angles = positions.astype(F32)[:, None] * inverse[None, :]
    cosine, sine = jnp.cos(angles), jnp.sin(angles)
    return jnp.concatenate([cosine, cosine], axis=1), jnp.concatenate([-sine, sine], axis=1)


def masked_scores(query, key, length, first):
    rows, keys = query.shape[0], key.shape[0]
    scores = dot_t(query, key) * (1.0 / math.sqrt(HD))
    at = first + lax.broadcasted_iota(jnp.int32, (rows, keys), 0)
    to = lax.broadcasted_iota(jnp.int32, (rows, keys), 1)
    return jnp.where((to <= at) & (to < length), scores, MASKED)


def attend_kernel(heads, kv_heads, tile, lengths, qkv_ref, cos_ref, sin_ref, att_ref, low_ref, lse_ref):
    length = lengths[pl.program_id(0)]
    full_len = qkv_ref.shape[0]
    for h in range(heads + kv_heads):
        cols = slice(h * HD, (h + 1) * HD)
        low_ref[:, cols] = rope(qkv_ref[:, cols], cos_ref[...], sin_ref[...]).astype(BF16)
    first_value = (heads + kv_heads) * HD
    low_ref[:, first_value:] = qkv_ref[:, first_value:].astype(BF16)
    lse_ref[...] = jnp.zeros_like(lse_ref)
    for first in range(0, full_len, tile):
        rows, keys = slice(first, first + tile), slice(0, first + tile)
        for h in range(heads):
            kv = h * kv_heads // heads
            key = low_ref[keys, (heads + kv) * HD : (heads + kv + 1) * HD]
            value = low_ref[keys, first_value + kv * HD : first_value + (kv + 1) * HD]
            scores = masked_scores(low_ref[rows, h * HD : (h + 1) * HD], key, length, first)
            largest = jnp.max(scores, axis=1, keepdims=True)
            exponent = jnp.exp(scores - largest)
            total = jnp.sum(exponent, axis=1, keepdims=True)
            probs = (exponent / total).astype(BF16)
            att_ref[rows, h * HD : (h + 1) * HD] = dot(probs, value).astype(BF16)
            lse_ref[rows, h : h + 1] = largest + jnp.log(total)


def attend_back_kernel(
    heads, kv_heads, tile, lengths, low_ref, lse_ref, g_ref, cos_ref, sin_ref, out_ref, k_acc, v_acc
):
    length = lengths[pl.program_id(0)]
    full_len = low_ref.shape[0]
    first_value = (heads + kv_heads) * HD
    scale = 1.0 / math.sqrt(HD)
    k_acc[...] = jnp.zeros_like(k_acc)
    v_acc[...] = jnp.zeros_like(v_acc)
    for first in range(0, full_len, tile):
        rows, keys = slice(first, first + tile), slice(0, first + tile)
        for h in range(heads):
            kv = h * kv_heads // heads
            kv_cols = slice(kv * HD, (kv + 1) * HD)
            key = low_ref[keys, (heads + kv) * HD : (heads + kv + 1) * HD]
            value = low_ref[keys, first_value + kv * HD : first_value + (kv + 1) * HD]
            query = low_ref[rows, h * HD : (h + 1) * HD]
            grad = g_ref[rows, h * HD : (h + 1) * HD]
            probs = jnp.exp(masked_scores(query, key, length, first) - lse_ref[rows, h : h + 1])
            g_probs = dot_t(grad, value)
            centre = jnp.sum(probs * g_probs, axis=1, keepdims=True)
            g_scores = (probs * (g_probs - centre)).astype(BF16)
            g_query = dot(g_scores, key) * scale
            out_ref[rows, h * HD : (h + 1) * HD] = rope(
                g_query, cos_ref[rows, :], -sin_ref[rows, :]
            ).astype(BF16)
            k_acc[keys, kv_cols] += token_sum(g_scores, query)
            v_acc[keys, kv_cols] += token_sum(probs.astype(BF16), grad)
    for kv in range(kv_heads):
        cols = slice(kv * HD, (kv + 1) * HD)
        out_ref[:, (heads + kv) * HD : (heads + kv + 1) * HD] = rope(
            k_acc[:, cols] * scale, cos_ref[...], -sin_ref[...]
        ).astype(BF16)
    out_ref[:, first_value:] = v_acc[...].astype(BF16)


def attention(qkv, lengths, groups, heads, kv_heads, tables):
    tokens, cols = qkv.shape
    full_len = tokens // groups
    tile = min(256, full_len)

    def seq(width):
        return pl.BlockSpec((full_len, width), lambda g, lens: (g, 0))

    table = pl.BlockSpec((full_len, HD), lambda g, lens: (0, 0))
    params = pltpu.CompilerParams(vmem_limit_bytes=56 * 1024 * 1024)
    att, low, lse = pl.pallas_call(
        functools.partial(attend_kernel, heads, kv_heads, tile),
        out_shape=(
            jax.ShapeDtypeStruct((tokens, heads * HD), BF16),
            jax.ShapeDtypeStruct((tokens, cols), BF16),
            jax.ShapeDtypeStruct((tokens, HD), F32),
        ),
        grid_spec=pltpu.PrefetchScalarGridSpec(
            num_scalar_prefetch=1,
            grid=(groups,),
            in_specs=[seq(cols), table, table],
            out_specs=[seq(heads * HD), seq(cols), seq(HD)],
        ),
        compiler_params=params,
        name="attend",
    )(lengths, qkv, *tables)

    def backward(grad):
        return pl.pallas_call(
            functools.partial(attend_back_kernel, heads, kv_heads, tile),
            out_shape=jax.ShapeDtypeStruct((tokens, cols), BF16),
            grid_spec=pltpu.PrefetchScalarGridSpec(
                num_scalar_prefetch=1,
                grid=(groups,),
                in_specs=[seq(cols), seq(HD), seq(heads * HD), table, table],
                out_specs=seq(cols),
                scratch_shapes=[
                    pltpu.VMEM((full_len, kv_heads * HD), F32),
                    pltpu.VMEM((full_len, kv_heads * HD), F32),
                ],
            ),
            compiler_params=params,
            name="attend_back",
        )(lengths, low, lse, grad, *tables)

    return att, backward


def ring_at(i, n):
    upper = i // (n // 2)
    return (1 - upper) * 2 * i + upper * (2 * (n - 1 - i) + 1)


def ring_pos(s, n):
    return (1 - s % 2) * (s // 2) + (s % 2) * (n - 1 - s // 2)


def greet(targets):
    barrier = pltpu.get_barrier_semaphore()
    for target in targets:
        pl.semaphore_signal(barrier, inc=1, device_id=target, device_id_type=MESH)
    pl.semaphore_wait(barrier, len(targets))


def send_to(source, target, send_sem, recv_sem, device):
    return pltpu.make_async_remote_copy(
        source, target, send_sem, recv_sem, device_id=device, device_id_type=MESH
    )


def xor(a, b, n):
    total, bit = 0, 1
    while bit < n:
        total = total + ((a // bit + b // bit) % 2) * bit
        bit *= 2
    return total


def home(q, z, k, n):
    return xor(xor(q, z, n), k * (n // 2), n)


def halves(ref, k):
    length = ref.shape[-2] // 2
    return pl.ds(k * length, length)


def others(n, n_c):
    me = lax.axis_index("shard") * n_c + lax.axis_index("context")
    peers = []
    for k in range(1, n * n_c):
        i = (me + k) % (n * n_c)
        peers.append({"shard": i // n_c, "context": i % n_c})
    return peers


class Exchange:
    def __init__(self, n, n_c, source, target, send_sem, recv_sem, own_sem, same):
        s, c = lax.axis_index("shard"), lax.axis_index("context")
        everyone = n * n_c
        me = s * n_c + c
        self.copies, self.arrivals = [], []
        for k, peer in enumerate(others(n, n_c), 1):
            to = (peer["shard"],) if same else (peer["shard"], peer["context"])
            self.copies.append(
                send_to(source.at[to], target.at[s, c], send_sem.at[k], recv_sem.at[k], peer)
            )
            i = (me + everyone - k) % everyone
            slot = target.at[i // n_c, i % n_c]
            self.arrivals.append(send_to(slot, slot, send_sem.at[k], recv_sem.at[k], peer))
        mine = source.at[s] if same else source.at[s, c]
        self.own = pltpu.make_async_copy(mine, target.at[s, c], own_sem.at[0])

    def start(self):
        for copy in self.copies:
            copy.start()
        self.own.start()

    def finish(self):
        self.own.wait()
        for copy in self.arrivals:
            copy.wait_recv()
        for copy in self.copies:
            copy.wait_send()

    @staticmethod
    def sems(n, n_c):
        dma = pltpu.SemaphoreType.DMA
        return [dma((n * n_c,)), dma((n * n_c,)), dma((1,))]


class Arrive:
    def __init__(self, n, source, middle, target, sems):
        self.s, self.c = lax.axis_index("shard"), lax.axis_index("context")
        self.to = [home(self.s, self.c, k, n) for k in (0, 1)]
        self.first, self.second, self.local = [], [], []
        for k in (0, 1):
            rows = halves(source, k)
            self.first.append(
                send_to(
                    source.at[rows], middle.at[rows], sems.at[0, k], sems.at[1, k],
                    {"shard": self.to[k]},
                )
            )
            self.second.append(
                send_to(
                    middle.at[rows], target.at[rows], sems.at[2, k], sems.at[3, k],
                    {"context": self.to[k]},
                )
            )
            self.local.append(
                (
                    pltpu.make_async_copy(source.at[rows], middle.at[rows], sems.at[4, k]),
                    pltpu.make_async_copy(middle.at[rows], target.at[rows], sems.at[5, k]),
                )
            )

    def either(self, stage, k, remote, local):
        own = self.s if stage == 0 else self.c
        pl.when(self.to[k] != own)(remote)
        pl.when(self.to[k] == own)(local)

    def start(self):
        for k in (0, 1):
            self.either(0, k, self.first[k].start, self.local[k][0].start)

    def relay(self):
        for k in (0, 1):
            self.either(0, k, self.first[k].wait_recv, self.local[k][0].wait)
            self.either(1, k, self.second[k].start, self.local[k][1].start)

    def finish(self):
        for k in (0, 1):
            self.either(0, k, self.first[k].wait_send, lambda: None)

            def both(copy=self.second[k]):
                copy.wait_send()
                copy.wait_recv()

            self.either(1, k, both, self.local[k][1].wait)

    @staticmethod
    def scratch(shape):
        return [pltpu.VMEM(shape, BF16), pltpu.SemaphoreType.DMA((6, 2))]


class Depart:
    def __init__(self, n, source, target, sems):
        s, c, t = (lax.axis_index(name) for name in ("shard", "context", "tensor"))
        self.stays, self.away, self.kept, self.passed, self.got = [], [], [], [], []
        for k in (0, 1):
            rows = halves(source, k)
            block = home(s, c, k, n)
            self.stays.append((s == c) & (block == s))
            self.away.append(
                send_to(
                    source.at[rows], target.at[t, rows], sems.at[0, k], sems.at[1, k],
                    {"shard": c, "context": block},
                )
            )
            self.kept.append(
                pltpu.make_async_copy(source.at[rows], target.at[t, rows], sems.at[4, k])
            )
            for core, group in ((t, self.passed), (1 - t, self.got)):
                spot = target.at[core, rows]
                group.append(
                    send_to(spot, spot, sems.at[2, k], sems.at[3, k], {"tensor": 1 - t})
                )

    def start(self):
        for k in (0, 1):
            pl.when(~self.stays[k])(self.away[k].start)
            pl.when(self.stays[k])(self.kept[k].start)

    def finish(self):
        for k in (0, 1):
            pl.when(~self.stays[k])(self.away[k].wait_recv)
            pl.when(self.stays[k])(self.kept[k].wait)
            self.passed[k].start()
        for k in (0, 1):
            self.got[k].wait_recv()
            self.passed[k].wait_send()
            pl.when(~self.stays[k])(self.away[k].wait_send)

    @staticmethod
    def sems():
        return [pltpu.SemaphoreType.DMA((5, 2))]


def neighbours(n):
    pos = ring_pos(lax.axis_index("shard"), n)
    sides = tuple({"shard": ring_at((pos + step) % n, n)} for step in (1, n - 1))
    return pos, sides, {"tensor": 1 - lax.axis_index("tensor")}


def ring_steps(n):
    half = n // 2
    steps = []
    for d in range(1, half + 1):
        steps += [(0, d, 0), (1, d, 1)]
        if d < half:
            steps += [(0, d, 1), (1, d, 0)]
    return steps


def gather_kernel(n, count, *refs):
    sources, outs = refs[:count], refs[count : 2 * count]
    ring_send, ring_recv, pair_send, pair_recv, own_sem = refs[2 * count :]
    half_len = sources[0].shape[0] // 2
    steps = ring_steps(n)
    t = lax.axis_index("tensor")
    pos, sides, partner = neighbours(n)
    greet(sides + (partner,))
    arrays = range(count)

    def rows(k):
        return pl.ds(k * half_len, half_len)

    layer = lax.axis_index("context")

    def place(a, core, who, k):
        return outs[a].at[core, home(ring_at(who % n, n), layer, k, n), rows(k)]

    def origin(way, d):
        return pos + (n - d if way == 0 else d)

    def sent(a, way, d, k):
        spot = place(a, t, origin(way, d - 1), k)
        source = sources[a].at[rows(k)] if d == 1 else spot
        at = (a, way, d - 1, k)
        return send_to(source, spot, ring_send.at[at], ring_recv.at[at], sides[way])

    def got(a, way, d, k):
        spot, at = place(a, t, origin(way, d), k), (a, way, d - 1, k)
        return send_to(spot, spot, ring_send.at[at], ring_recv.at[at], sides[way])

    def pair(a, core, way, d, k, source=None):
        spot, at = place(a, core, origin(way, d), k), (a, way, d, k)
        return send_to(
            spot if source is None else source, spot, pair_send.at[at], pair_recv.at[at], partner
        )

    waits = []
    for step in steps:
        if step[1] == 1:
            for a in arrays:
                waits.append(sent(a, *step))
                waits[-1].start()
    own = []
    for a in arrays:
        for k in (0, 1):
            waits.append(pair(a, t, 0, 0, k, sources[a].at[rows(k)]))
            waits[-1].start()
            own.append(
                pltpu.make_async_copy(sources[a].at[rows(k)], place(a, t, pos, k), own_sem.at[a, k])
            )
            own[-1].start()
    for way, d, k in steps:
        for a in arrays:
            got(a, way, d, k).wait_recv()
            if (way, d + 1, k) in steps:
                waits.append(sent(a, way, d + 1, k))
                waits[-1].start()
            waits.append(pair(a, t, way, d, k))
            waits[-1].start()
    for a in arrays:
        for step in [(0, 0, 0), (0, 0, 1)] + steps:
            pair(a, 1 - t, *step).wait_recv()
    for copy in waits:
        copy.wait_send()
    for copy in own:
        copy.wait()


def gather_tokens(call, *values):
    n, count, half = lax.axis_size("shard"), len(values), lax.axis_size("shard") // 2
    dma = pltpu.SemaphoreType.DMA
    outs = pl.pallas_call(
        functools.partial(gather_kernel, n, count),
        out_shape=[jax.ShapeDtypeStruct((2, n) + v.shape, v.dtype) for v in values],
        in_specs=[pl.BlockSpec(memory_space=pltpu.VMEM)] * count,
        out_specs=[pl.BlockSpec(memory_space=pl.ANY)] * count,
        scratch_shapes=[
            dma((count, 2, half, 2)),
            dma((count, 2, half, 2)),
            dma((count, 2, half + 1, 2)),
            dma((count, 2, half + 1, 2)),
            dma((count, 2)),
        ],
        compiler_params=pltpu.CompilerParams(collective_id=call, has_side_effects=True),
        cost_estimate=pl.CostEstimate(flops=0, bytes_accessed=100_000_000, transcendentals=0),
        name=f"gather_{call}",
    )(*values)
    return [out.reshape(2 * n * v.shape[0], v.shape[1]) for out, v in zip(outs, values)]


def scatter_tokens(call, *values, depart=None, exits=None):
    n, n_c, count = lax.axis_size("shard"), lax.axis_size("context"), len(values)
    cols = sum(v.shape[1] for v in values)
    length = values[0].shape[0] // (2 * n)
    half, half_len = n // 2, length // 2
    steps = ring_steps(n)

    def kernel(*refs):
        refs = list(refs)
        parts = [refs.pop(0) for _ in range(count)]
        depart_ref = refs.pop(0) if depart is not None else None
        exits_ref = refs.pop(0) if exits is not None else None
        out_ref = refs.pop(0)
        depart_out = refs.pop(0) if depart is not None else None
        exits_out = refs.pop(0) if exits is not None else None
        mine, other, outbox, inbox = [refs.pop(0) for _ in range(4)]
        ring_send, ring_recv, pair_send, pair_recv, load_sem = [refs.pop(0) for _ in range(5)]
        t = lax.axis_index("tensor")
        layer = lax.axis_index("context")
        pos, sides, partner = neighbours(n)
        jobs = []
        if depart is not None:
            jobs.append(Depart(n, depart_ref, depart_out, refs.pop(0)))
        if exits is not None:
            exits_in = refs.pop(0)
            jobs.append(
                Exchange(n, n_c, exits_ref, exits_in, *(refs.pop(0) for _ in range(3)), False)
            )
        greet((others(n, n_c) if jobs else list(sides)) + [partner])
        order = [half]
        for d in range(half - 1, 0, -1):
            order += [d, n - d]
        order.append(0)

        def rows(k):
            return pl.ds(k * half_len, half_len)

        swaps, loads = {}, {}
        for d in order:
            who = ring_at((pos + d) % n, n)
            swaps[d], loads[d], first = [], [], 0
            for a, part in enumerate(parts):
                cols_a = pl.ds(first, part.shape[-1])
                first += part.shape[-1]
                for k in (0, 1):
                    at = (a, d, k)
                    block = home(who, layer, k, n)
                    loads[d].append(
                        pltpu.make_async_copy(
                            part.at[t, block, rows(k)], mine.at[d, rows(k), cols_a], load_sem.at[at]
                        )
                    )
                    swaps[d].append(
                        send_to(
                            part.at[1 - t, block, rows(k)], other.at[d, rows(k), cols_a],
                            pair_send.at[at], pair_recv.at[at], partner,
                        )
                    )
                    swaps[d][-1].start()
                    loads[d][-1].start()
        for job in jobs:
            job.start()

        def ready(d):
            for copy in loads[d]:
                copy.wait()
            for copy in swaps[d]:
                copy.wait_recv()

        def chip_sum(d, k):
            return mine[d, rows(k), :].astype(F32) + other[d, rows(k), :].astype(F32)

        def ring(way, d, k):
            at = (way, d - 1, k)
            box = (way, d - 1, rows(k))
            return send_to(
                outbox.at[box], inbox.at[box], ring_send.at[at], ring_recv.at[at], sides[way]
            )

        def send(way, d, k, total):
            outbox[way, d - 1, rows(k), :] = total.astype(BF16)
            ring(way, d, k).start()

        def taken(way, d, k):
            ring(way, d, k).wait_recv()
            return inbox[way, d - 1, rows(k), :].astype(F32)

        ready(half)
        send(0, half, 0, chip_sum(half, 0))
        send(1, half, 1, chip_sum(half, 1))
        for d in range(half - 1, 0, -1):
            for way, index in ((0, d), (1, n - d)):
                ready(index)
                k = 1 - way
                total = chip_sum(index, k)
                if (way, d + 1, k) in steps:
                    total = total + taken(way, d + 1, k)
                send(way, d, k, total)
            for way, index in ((0, d), (1, n - d)):
                send(way, d, way, chip_sum(index, way) + taken(way, d + 1, way))
        ready(0)
        for k in (0, 1):
            out_ref[rows(k), :] = chip_sum(0, k)
        for way, k in ((0, 1), (1, 0), (0, 0), (1, 1)):
            out_ref[rows(k), :] += taken(way, 1, k)
        for step in steps:
            ring(*step).wait_send()
        for d in order:
            for copy in swaps[d]:
                copy.wait_send()
        for job in jobs:
            job.finish()
        if exits is not None:
            add_layers(exits_in, exits_out)

    dma = pltpu.SemaphoreType.DMA
    any_space, vmem = pl.BlockSpec(memory_space=pl.ANY), pl.BlockSpec(memory_space=pltpu.VMEM)
    operands = [v.astype(BF16).reshape(2, n, length, v.shape[1]) for v in values]
    in_specs, out_specs = [any_space] * count, [vmem]
    out_shape = [jax.ShapeDtypeStruct((length, cols), F32)]
    scratch = [
        pltpu.VMEM((n, length, cols), BF16),
        pltpu.VMEM((n, length, cols), BF16),
        pltpu.VMEM((2, half, length, cols), BF16),
        pltpu.VMEM((2, half, length, cols), BF16),
        dma((2, half, 2)),
        dma((2, half, 2)),
        dma((count, n, 2)),
        dma((count, n, 2)),
        dma((count, n, 2)),
    ]
    if depart is not None:
        operands.append(depart)
        in_specs.append(vmem)
        out_specs.append(any_space)
        out_shape.append(jax.ShapeDtypeStruct((2,) + depart.shape, BF16))
        scratch += Depart.sems()
    if exits is not None:
        operands.append(exits)
        in_specs.append(vmem)
        out_specs.append(vmem)
        out_shape.append(jax.ShapeDtypeStruct((n,) + exits.shape[2:], F32))
        scratch += [pltpu.VMEM(exits.shape, BF16)] + Exchange.sems(n, n_c)
    return pl.pallas_call(
        kernel,
        out_shape=out_shape,
        in_specs=in_specs,
        out_specs=out_specs,
        scratch_shapes=scratch,
        compiler_params=pltpu.CompilerParams(
            collective_id=call, has_side_effects=True, vmem_limit_bytes=52 * 1024 * 1024
        ),
        cost_estimate=pl.CostEstimate(flops=0, bytes_accessed=100_000_000, transcendentals=0),
        name=f"scatter_{call}",
    )(*operands)


def add_layers(inbox, out_ref):
    for q in range(inbox.shape[0]):
        total = inbox[q, 0].astype(F32)
        for i in range(1, inbox.shape[1]):
            total = total + inbox[q, i].astype(F32)
        out_ref[q] = total


def spread(call, sources, items, widths, tokens, wide=None):
    n, n_c = lax.axis_size("shard"), lax.axis_size("context")
    n_in, n_out = len(sources), len(widths)
    rows = sources[0].shape[0]

    def kernel(*refs):
        refs = list(refs)
        ins = [refs.pop(0) for _ in range(n_in)]
        tokens_ref = refs.pop(0)
        wide_ref = refs.pop(0) if wide is not None else None
        outs = [refs.pop(0) for _ in range(n_out)]
        tokens_out = refs.pop(0)
        wide_out = refs.pop(0) if wide is not None else None
        send_sem, recv_sem, own_sem = refs.pop(0), refs.pop(0), refs.pop(0)
        arrive = Arrive(n, tokens_ref, refs.pop(0), tokens_out, refs.pop(0))
        s = lax.axis_index("shard")
        exchange = None
        if wide is not None:
            exchange = Exchange(
                n, n_c, wide_ref, wide_out, *(refs.pop(0) for _ in range(3)), True
            )
        bounce = refs
        greet(others(n, n_c))

        def piece(item, q):
            source, _, _, width, kind, heads = items[item]
            if kind == "split":
                first = pl.multiple_of(q * width, HD)
            elif kind == "kv":
                first = pl.multiple_of((q * heads // n) * HD, HD)
            else:
                first = 0
            return ins[source].at[:, pl.ds(first, width)]

        def spot(item, q):
            _, out, first, width, _, _ = items[item]
            return outs[out].at[q, :, pl.ds(first, width)]

        arrive.start()
        waits, own, arrivals = [], [], []
        for item in range(len(items)):
            for k in range(1, n):
                q = (s + k) % n
                at = (item, k)
                copy = send_to(
                    piece(item, q), spot(item, s), send_sem.at[at], recv_sem.at[at], {"shard": q}
                )
                copy.start()
                waits.append(copy)
                q = (s + n - k) % n
                arrivals.append(
                    send_to(
                        spot(item, q), spot(item, q), send_sem.at[at], recv_sem.at[at], {"shard": q}
                    )
                )
            copy = pltpu.make_async_copy(piece(item, s), bounce[item], own_sem.at[item, 0])
            copy.start()
            own.append(copy)
        if exchange is not None:
            exchange.start()
        stored = []
        for item in range(len(items)):
            own[item].wait()
            copy = pltpu.make_async_copy(bounce[item], spot(item, s), own_sem.at[item, 1])
            copy.start()
            stored.append(copy)
        arrive.relay()
        for copy in stored:
            copy.wait()
        if exchange is not None:
            exchange.finish()
        for copy in arrivals:
            copy.wait_recv()
        for copy in waits:
            copy.wait_send()
        arrive.finish()

    dma = pltpu.SemaphoreType.DMA
    any_space, vmem = pl.BlockSpec(memory_space=pl.ANY), pl.BlockSpec(memory_space=pltpu.VMEM)
    scratch = [dma((len(items), n)), dma((len(items), n)), dma((len(items), 2))]
    scratch += Arrive.scratch(tokens.shape)
    out_shape = [jax.ShapeDtypeStruct((n, rows, w), BF16) for w in widths]
    out_shape.append(jax.ShapeDtypeStruct(tokens.shape, BF16))
    operands = list(sources) + [tokens]
    if wide is not None:
        operands.append(wide)
        scratch += Exchange.sems(n, n_c)
        out_shape.append(jax.ShapeDtypeStruct((n, n_c) + wide.shape[1:], BF16))
    scratch += [pltpu.VMEM((rows, item[3]), BF16) for item in items]
    return pl.pallas_call(
        kernel,
        out_shape=out_shape,
        in_specs=[any_space] * n_in + [vmem] * (len(operands) - n_in),
        out_specs=[any_space] * len(out_shape),
        scratch_shapes=scratch,
        compiler_params=pltpu.CompilerParams(collective_id=call, has_side_effects=True),
        cost_estimate=pl.CostEstimate(flops=0, bytes_accessed=40_000_000, transcendentals=0),
        name=f"spread_{call}",
    )(*operands)


def collect(call, exits, rows, depart):
    n, n_c = exits.shape[:2]

    def kernel(
        exits_ref, rows_ref, depart_ref, exits_out, rows_out, depart_out, exits_in, rows_in, *sems
    ):
        c = lax.axis_index("context")
        leave = Depart(n, depart_ref, depart_out, sems[0])
        exchange = Exchange(n, n_c, exits_ref, exits_in, *sems[1:4], False)
        greet(others(n, n_c) + [{"tensor": 1 - lax.axis_index("tensor")}])
        leave.start()
        waits, arrivals = [], []
        for k in range(1, n_c):
            to, via = (c + k) % n_c, (c + n_c - k) % n_c
            at = (sems[4].at[0, k], sems[4].at[1, k])
            waits.append(send_to(rows_ref.at[to], rows_in.at[c], *at, {"context": to}))
            waits[-1].start()
            arrivals.append(send_to(rows_in.at[via], rows_in.at[via], *at, {"context": to}))
        exchange.start()
        kept = pltpu.make_async_copy(rows_ref.at[c], rows_in.at[c], sems[4].at[0, 0])
        kept.start()
        kept.wait()
        for copy in arrivals:
            copy.wait_recv()
        total = rows_in[0].astype(F32)
        for i in range(1, n_c):
            total = total + rows_in[i].astype(F32)
        rows_out[...] = total
        exchange.finish()
        add_layers(exits_in, exits_out)
        leave.finish()
        for copy in waits:
            copy.wait_send()

    vmem = pl.BlockSpec(memory_space=pltpu.VMEM)
    return pl.pallas_call(
        kernel,
        out_shape=(
            jax.ShapeDtypeStruct((n,) + exits.shape[2:], F32),
            jax.ShapeDtypeStruct(rows.shape[1:], F32),
            jax.ShapeDtypeStruct((2,) + depart.shape, BF16),
        ),
        in_specs=[vmem] * 3,
        out_specs=(vmem, vmem, pl.BlockSpec(memory_space=pl.ANY)),
        scratch_shapes=[pltpu.VMEM(exits.shape, BF16), pltpu.VMEM(rows.shape, BF16)]
        + Depart.sems()
        + Exchange.sems(n, n_c)
        + [pltpu.SemaphoreType.DMA((2, n_c))],
        compiler_params=pltpu.CompilerParams(collective_id=call, has_side_effects=True),
        cost_estimate=pl.CostEstimate(flops=0, bytes_accessed=60_000_000, transcendentals=0),
        name=f"collect_{call}",
    )(exits, rows, depart)


def entry_grads(pairs, n_s, n_c, s):
    tokens, width = pairs[0][0].shape
    block = width // (n_s * n_c)
    if block % HD:
        parts = []
        for acts, side in pairs:
            mine = lax.dynamic_index_in_dim(
                acts.reshape(tokens, n_c, n_s, block), s, 2, keepdims=False
            )
            parts.append(token_sum(mine.reshape(tokens, n_c * block), side))
        return jnp.concatenate(parts, axis=1).astype(BF16).reshape(n_c, block, -1)
    count = len(pairs)
    total = sum(side.shape[1] for _, side in pairs)

    def kernel(_, *refs):
        first = 0
        for a in range(count):
            cols = slice(first, first + refs[count + a].shape[1])
            first = cols.stop
            refs[-1][0, :, cols] = token_sum(refs[a][...], refs[count + a][...]).astype(BF16)

    return pl.pallas_call(
        kernel,
        out_shape=jax.ShapeDtypeStruct((n_c, block, total), BF16),
        grid_spec=pltpu.PrefetchScalarGridSpec(
            num_scalar_prefetch=1,
            grid=(n_c,),
            in_specs=[pl.BlockSpec((tokens, block), lambda i, at: (0, i * n_s + at[0]))] * count
            + [pl.BlockSpec(side.shape, lambda i, at: (0, 0)) for _, side in pairs],
            out_specs=pl.BlockSpec((1, block, total), lambda i, at: (i, 0, 0)),
        ),
        name="entry_grads",
    )(s.reshape(1).astype(jnp.int32), *(a for a, _ in pairs), *(b for _, b in pairs))


def shards(
    hidden_in,
    cotangent,
    seq_lengths,
    adapter_ids,
    attn_gain,
    ffn_gain,
    query_weight,
    key_weight,
    value_weight,
    output_weight,
    gate_weight,
    up_weight,
    down_weight,
    qkv_entry,
    query_exit,
    key_exit,
    value_exit,
    attn_entry,
    attn_exit,
    gate_entry,
    gate_exit,
    up_entry,
    up_exit,
    down_entry,
    down_exit,
):
    n_s, n_c = lax.axis_size("shard"), lax.axis_size("context")
    s, t = lax.axis_index("shard"), lax.axis_index("tensor")
    groups, local_len, width = hidden_in.shape
    block = width // (n_s * n_c)
    full_len = local_len * n_c
    tokens = groups * full_len
    ranks = qkv_entry.shape[1]
    swap = [(a * n_c + b, b * n_c + a) for a in range(n_s) for b in range(n_c)]

    def own_tokens(values):
        own = lax.dynamic_index_in_dim(values, t, 0, keepdims=False)
        own = own.reshape(local_len, n_s, n_c, block).transpose(0, 2, 1, 3)
        return own.reshape(local_len, width)

    def as_output(values):
        swapped = values.reshape(2, local_len, n_c, n_s, block).transpose(0, 1, 3, 2, 4)
        return swapped.reshape(2, local_len, width)

    def features(vector):
        return vector.reshape(n_s, n_c, block).transpose(1, 0, 2).reshape(width).astype(F32)

    q_cols = query_weight.shape[1] // n_s
    f_cols = gate_weight.shape[1] // n_s
    kv_here = key_weight.shape[1] // HD
    kv_take = max(1, kv_here // n_s)
    k_cols = kv_take * HD
    heads = q_cols // HD
    a_cols = q_cols + 2 * k_cols

    def split(weights):
        rows, cols = weights.shape
        return weights.reshape(rows, n_s, cols // n_s).transpose(1, 0, 2)

    def split_kv(weights):
        first = [q * kv_here // n_s * HD for q in range(n_s)]
        return jnp.stack([weights[:, at : at + k_cols] for at in first])

    exit_pack = jnp.concatenate(
        [
            split(query_exit),
            split_kv(key_exit),
            split_kv(value_exit),
            split(attn_entry),
            split(gate_exit),
            split(up_exit),
            split(down_entry),
        ],
        axis=2,
    )
    entry_a = jnp.where(t == 0, qkv_entry, attn_exit)
    entry_f = jnp.where(t == 0, gate_entry, up_entry)
    attn_pack, x_low, exits = spread(
        0,
        [query_weight, key_weight, value_weight, output_weight, entry_a],
        [
            (0, 0, 0, q_cols, "split", 0),
            (1, 0, q_cols, k_cols, "kv", kv_here),
            (2, 0, q_cols + k_cols, k_cols, "kv", kv_here),
            (3, 0, a_cols, q_cols, "split", 0),
            (4, 0, a_cols + q_cols, ranks, "same", 0),
        ],
        [a_cols + q_cols + ranks],
        own_tokens(hidden_in),
        exit_pack,
    )
    gu_pack, down_pack, cot_low = spread(
        1,
        [gate_weight, up_weight, entry_f, down_exit, down_weight],
        [
            (0, 0, 0, f_cols, "split", 0),
            (1, 0, f_cols, f_cols, "split", 0),
            (2, 0, 2 * f_cols, ranks, "same", 0),
            (3, 0, 2 * f_cols + ranks, ranks, "same", 0),
            (4, 1, 0, f_cols, "split", 0),
        ],
        [2 * f_cols + 2 * ranks, f_cols],
        own_tokens(cotangent),
    )

    def along(pack):
        return lax.all_gather(pack, "context", axis=0).reshape(width, -1)

    def both_cores(mine):
        theirs = lax.ppermute(mine, "tensor", [(0, 1), (1, 0)])
        return jnp.where(t == 0, mine, theirs), jnp.where(t == 0, theirs, mine)

    attn_w = along(attn_pack)
    gu_w = along(gu_pack)
    w_d = along(down_pack)
    exits = exits.reshape(ranks, -1)
    lengths, ids = lax.ppermute(
        jnp.stack([seq_lengths, adapter_ids]), ("shard", "context"), swap
    )
    gain_one, gain_two = features(attn_gain), features(ffn_gain)
    layer, part_len = lax.axis_index("context"), local_len // 2
    positions = jnp.concatenate(
        [
            home(s, layer, k, n_s) * local_len + k * part_len + jnp.arange(part_len)
            for k in (0, 1)
        ]
    )
    valid = (positions < lengths[t]).astype(F32)[:, None]
    chosen = (jnp.arange(ranks)[None, :] // RANK == ids[:, None]).astype(F32)
    select_own = chosen[t][None, :]
    select_all = jnp.broadcast_to(chosen[:, None, :], (groups, full_len, ranks)).reshape(
        tokens, ranks
    )
    w_qkv, w_o = attn_w[:, :a_cols], attn_w[:, a_cols : a_cols + q_cols]
    e_qkv, e_o = exits[:, :a_cols], exits[:, a_cols : a_cols + q_cols]
    qkv_in, attn_out = both_cores(attn_w[:, a_cols + q_cols :])
    w_g, w_u = gu_w[:, :f_cols], gu_w[:, f_cols : 2 * f_cols]
    gate_in, up_in = both_cores(gu_w[:, 2 * f_cols : 2 * f_cols + ranks])
    down_out = gu_w[:, 2 * f_cols + ranks :]
    e_g, e_u, e_d = (
        exits[:, a_cols + q_cols + i * f_cols : a_cols + q_cols + (i + 1) * f_cols]
        for i in range(3)
    )

    inputs = x_low.astype(F32)
    (n1,) = gather_tokens(2, rms_scale(inputs, gain_one).astype(BF16))
    en_qkv = (select_all * dot(n1, qkv_in)).astype(BF16)
    qkv = dot(n1, w_qkv) + dot(en_qkv, e_qkv)
    att, attention_back = attention(
        qkv, lengths, groups, heads, kv_take, head_tables(jnp.arange(full_len))
    )
    (total,) = scatter_tokens(3, dot_t(att, w_o), dot_t(att, e_o))
    en_attn = (select_own * total[:, width:]).astype(BF16)
    mid = inputs + total[:, :width] + dot_t(en_attn, attn_out)

    n2, en_attn_all = gather_tokens(4, rms_scale(mid, gain_two).astype(BF16), en_attn)
    en_gate = (select_all * dot(n2, gate_in)).astype(BF16)
    en_up = (select_all * dot(n2, up_in)).astype(BF16)
    gate = dot(n2, w_g) + dot(en_gate, e_g)
    up = dot(n2, w_u) + dot(en_up, e_u)
    sig = jax.nn.sigmoid(gate)
    hidden = (gate * sig * up).astype(BF16)
    (total,) = scatter_tokens(5, dot_t(hidden, w_d), dot_t(hidden, e_d))
    en_down = (select_own * total[:, width:]).astype(BF16)
    layer_sum = mid + total[:, :width] + dot_t(en_down, down_out)
    out_low = (valid * layer_sum).astype(BF16)

    grad_out = valid * cot_low.astype(F32)
    (g_low,) = gather_tokens(6, grad_out.astype(BF16))
    g_en_down = (select_all * dot(g_low, down_out)).astype(BF16)
    down_entry_grad = token_sum(g_en_down, hidden)
    g_hidden = dot(g_low, w_d) + dot(g_en_down, e_d)
    g_gate = (g_hidden * up * (sig * (1.0 + gate * (1.0 - sig)))).astype(BF16)
    g_up = (g_hidden * gate * sig).astype(BF16)
    gate_exit_grad = token_sum(en_gate, g_gate)
    up_exit_grad = token_sum(en_up, g_up)
    total, layer_out = scatter_tokens(
        7,
        dot_t(g_gate, w_g) + dot_t(g_up, w_u),
        dot_t(g_gate, e_g),
        dot_t(g_up, e_u),
        depart=out_low,
    )
    g_en_gu = (
        jnp.concatenate([select_own, select_own], axis=1) * total[:, width:]
    ).astype(BF16)
    g_two = (
        total[:, :width]
        + dot_t(g_en_gu[:, :ranks], gate_in)
        + dot_t(g_en_gu[:, ranks:], up_in)
    )
    g_mid = grad_out + norm_back(mid, gain_two, g_two)
    g_mid_all, side = gather_tokens(
        8, g_mid.astype(BF16), jnp.concatenate([g_en_gu, en_down], axis=1)
    )
    rows_mid = entry_grads(
        [(n2, side[:, : 2 * ranks]), (g_low, side[:, 2 * ranks :]), (g_mid_all, en_attn_all)],
        n_s,
        n_c,
        s,
    )

    g_en_attn = (select_all * dot(g_mid_all, attn_out)).astype(BF16)
    attn_entry_grad = token_sum(g_en_attn, att)
    g_att = (dot(g_mid_all, w_o) + dot(g_en_attn, e_o)).astype(BF16)
    g_qkv = attention_back(g_att)
    qkv_exit_grad = token_sum(en_qkv, g_qkv)
    per = ranks // (n_s * n_c)

    def by_owner(*grads):
        packed = jnp.concatenate([grad.astype(BF16) for grad in grads], axis=1)
        return packed.reshape(n_s, n_c, per, -1)

    total, ffn_grads = scatter_tokens(
        9,
        dot_t(g_qkv, w_qkv),
        dot_t(g_qkv, e_qkv),
        exits=by_owner(gate_exit_grad, up_exit_grad, down_entry_grad),
    )
    g_en_qkv = (select_own * total[:, width:]).astype(BF16)
    g_one = total[:, :width] + dot_t(g_en_qkv, qkv_in)
    in_low = (g_mid + norm_back(inputs, gain_one, g_one)).astype(BF16)
    (g_en_qkv_all,) = gather_tokens(10, g_en_qkv)
    rows_first = entry_grads([(n1, g_en_qkv_all)], n_s, n_c, s)

    attn_grads, rows, input_grad = collect(
        11,
        by_owner(qkv_exit_grad, attn_entry_grad),
        jnp.concatenate([rows_first, rows_mid], axis=2),
        in_low,
    )

    def join(grads, first, count):
        part = grads[:, :, first : first + count]
        return part.transpose(1, 0, 2).reshape(per, n_s * count)

    def join_kv(first):
        part = attn_grads[:, :, first : first + k_cols]
        copies = n_s * kv_take // kv_here
        part = part.reshape(n_s // copies, copies, per, k_cols).sum(axis=1)
        return part.transpose(1, 0, 2).reshape(per, kv_here * HD)

    qkv_eg, gate_eg, up_eg, down_xg, attn_xg = (
        rows[:, i * ranks : (i + 1) * ranks] for i in range(5)
    )
    return (
        as_output(layer_out),
        as_output(input_grad),
        qkv_eg,
        join(attn_grads, 0, q_cols),
        join_kv(q_cols),
        join_kv(q_cols + k_cols),
        join(attn_grads, a_cols, q_cols),
        attn_xg,
        gate_eg,
        join(ffn_grads, 0, f_cols),
        up_eg,
        join(ffn_grads, f_cols, f_cols),
        join(ffn_grads, 2 * f_cols, f_cols),
        down_xg,
    )


def solution(mesh):
    in_specs = (
        P("shard", "context", None),
        P("shard", "context", None),
        P("shard"),
        P("shard"),
        P(),
        P(),
        P(("shard", "context"), "tensor"),
        P(("shard", "context"), "tensor"),
        P(("shard", "context"), "tensor"),
        P(("shard", "context"), "tensor"),
        P(("shard", "context"), "tensor"),
        P(("shard", "context"), "tensor"),
        P(("shard", "context"), "tensor"),
        P(("shard", "context"), None),
        P(("shard", "context"), "tensor"),
        P(("shard", "context"), "tensor"),
        P(("shard", "context"), "tensor"),
        P(("shard", "context"), "tensor"),
        P(("shard", "context"), None),
        P(("shard", "context"), None),
        P(("shard", "context"), "tensor"),
        P(("shard", "context"), None),
        P(("shard", "context"), "tensor"),
        P(("shard", "context"), "tensor"),
        P(("shard", "context"), None),
    )
    out_specs = (
        P("shard", "context", None),
        P("shard", "context", None),
        P(("shard", "context"), None),
        P(("shard", "context"), "tensor"),
        P(("shard", "context"), "tensor"),
        P(("shard", "context"), "tensor"),
        P(("shard", "context"), "tensor"),
        P(("shard", "context"), None),
        P(("shard", "context"), None),
        P(("shard", "context"), "tensor"),
        P(("shard", "context"), None),
        P(("shard", "context"), "tensor"),
        P(("shard", "context"), "tensor"),
        P(("shard", "context"), None),
    )
    return jax.shard_map(shards, mesh=mesh, in_specs=in_specs, out_specs=out_specs, check_vma=False)
```

time: 1490 us -> 936 us (0.63)
  waiting for transfers between devices: 793 us -> 14.7 us
  Pallas kernels: 0 us -> 637 us
  blocking collectives: 224 us -> 0 us
  matrix products: 246 us -> 186 us
  local copies, waits for them, and re-layouts: 106 us -> 47.5 us
  other arithmetic: 71.3 us -> 25.3 us
  starting transfers between devices: 24.9 us -> 1.31 us
    pallas_call x0 -> x16, Pallas kernels: none -> 637 us  [the longest x4 211 us: scatter_tokens(): pl.pallas_call(kernel, out_shape=out_shape, in_specs=in_specs, out_specs=...]
    all_gather x9 -> x3, waiting for transfers between devices: 413 us -> 14 us  [along(): return lax.all_gather(pack, 'context', axis=0).reshape(width, -1)]
    reduce_scatter x5 -> x0, waiting for transfers between devices: 281 us -> none  [the longest x4 256 us: scatter_tokens(): lax.psum_scatter(values.astype(BF16), PLANE, scatter_dimension=0, tiled=T...]
    all_to_all x3 -> x0, blocking collectives: 167 us -> none  [spread(): swapped = lax.all_to_all(pieces, 'shard', 0, 0, tiled=True)]
    unnamed x16 -> x3, waiting for transfers between devices: 96.5 us -> 0.71 us
    all_gather x3 -> x0, blocking collectives: 57.2 us -> none  [the longest x2 32.4 us: spread(): return lax.all_gather(swapped, 'context', axis=0)]
    dot_general x6 -> x0, matrix products: 46.9 us -> none  [the longest x1 15.9 us: shards(): jnp.einsum('gqcrd,gkcd->gcrqk', g_heads, value, preferred_element_type=F32)]
    unnamed x229 -> x114, local copies, waits for them, and re-layouts: 34.9 us -> 7.11 us
  transfers between devices with their start and end apart: 22 -> 6, of which waited for: 13 -> 1; matrix products, arithmetic and copies ran while one was open for 12% -> 6% of each run, Pallas kernels for 0% -> 29%
where the time goes in v1:
time: 936 us; the launch traced here: 927 us
  Pallas kernels  637 us (68%)
  matrix products  186 us (20%)
  local copies, waits for them, and re-layouts  47.5 us (5%)
  other arithmetic  25.3 us (3%)
  between operations  15.2 us (2%)
  waiting for transfers between devices  14.7 us (2%)
    pallas_call x4, Pallas kernels, scatter_tokens(): pl.pallas_call(kernel, out_shape=out_shape, in_specs=in_specs, out_specs=...  211 us
    pallas_call x5, Pallas kernels, gather_tokens(): pl.pallas_call(functools.partial(gather_kernel, n, count), out_shape=[jax...  188 us
    pallas_call x2, Pallas kernels, spread(): pl.pallas_call(kernel, out_shape=out_shape, in_specs=[any_space] * n_in +...  142 us
    dot_general x15, matrix products, dot(): return jnp.dot(left, right, preferred_element_type=F32)  101 us
    dot_general x15, matrix products, dot_t(): lax.dot_general(left, right, (((1,), (1,)), ((), ())), preferred_element_...  77.7 us
    pallas_call x1, Pallas kernels, collect(): pl.pallas_call(kernel, out_shape=(jax.ShapeDtypeStruct((n,) + exits.shape...  56.5 us
  transfers between devices with their start and end apart: 6, of which 1 were waited for; matrix products, arithmetic and copies ran while one was open for 6% of the time, Pallas kernels for 29%

profile of v1, /device:TPU:0, one launch (start us, length us, event | category | flops | bytes accessed | tf_op | source)
XLA Modules:
  0.0 927.0 jit_solution(1783396481865843045)
XLA Ops:
  10.6 1.7 constant_dynamic-slice_fusion.1
  14.0 1.6 reshape.328.refs_5_
  18.7 1.5 broadcast_select_fusion.12
  20.1 58.5 %spread_0.1 = (bf16[4,128,896]{2,1,0:T(8,128)(2,1)}, bf16[256,2048]{1,0:T(8,128)(2,1)}, bf16[4,4,8,3840]{3,2,1,0:T(8,128)(2,1)}) custom-call(bf16[128,1024]{1,0:T(8,128)(2,1)} %refs_0_.3, bf16[128,512]{1,0:T(8,128)(2,1)} %refs_1_.3, bf16[128,512]{1,0:T(8,128)(2,1)} %refs_2_.1, bf16[128,1024]{1,0:T(8,128)(2,1)} %refs_3_.3, ...), custom_call_target="tpu_custom_call" | custom-call | bytes 40000000 | tf_op jit(solution)/shard_map/spread_0/pallas_call | solution.py:713
  80.3 1.6 reshape.322.refs_5_
  81.9 84.0 %spread_1.1 = (bf16[4,128,2304]{2,1,0:T(8,128)(2,1)}, bf16[4,128,1024]{2,1,0:T(8,128)(2,1)}, bf16[256,2048]{1,0:T(8,128)(2,1)}) custom-call(bf16[128,4096]{1,0:T(8,128)(2,1)} %refs_0_.2, bf16[128,4096]{1,0:T(8,128)(2,1)} %refs_1_.2, bf16[128,128]{1,0:T(8,128)(2,1)} %get-tuple-element.92.refs_2_, bf16[128,128]{1,0:T(8,128)(2,1)} %refs_3_.2, ...), custom_call_target="tpu_custom_call" | custom-call | bytes 40000000 | tf_op jit(solution)/shard_map/spread_1/pallas_call | solution.py:713
  170.3 44.3 %gather_2.1 = bf16[2,4,256,2048]{3,2,1,0:T(8,128)(2,1)} custom-call(bf16[256,2048]{1,0:T(8,128)(2,1)} %fusion.18.refs_0_), custom_call_target="tpu_custom_call" | custom-call | bytes 100000000 | tf_op jit(solution)/shard_map/gather_2/pallas_call | solution.py:440
  214.7 1.9 fusion.42
  220.9 41.0 %gather_6.1 = bf16[2,4,256,2048]{3,2,1,0:T(8,128)(2,1)} custom-call(bf16[256,2048]{1,0:T(8,128)(2,1)} %fusion.23.refs_0_), custom_call_target="tpu_custom_call" | custom-call | bytes 100000000 | tf_op jit(solution)/shard_map/gather_6/pallas_call | solution.py:440
  264.4 9.2 fusion.25
  273.6 2.4 fusion.12
  276.0 3.8 convolution_add_fusion.3.qkv_ref
  279.8 12.4 %attend.1 = (bf16[2048,256]{1,0:T(8,128)(2,1)}, bf16[2048,512]{1,0:T(8,128)(2,1)}, f32[2048,128]{1,0:T(8,128)}) custom-call(s32[2]{0:T(128)} %get-tuple-element.83.lengths, f32[2048,512]{1,0:T(8,128)} %convolution_add_fusion.3.qkv_ref, f32[1024,128]{1,0:T(8,128)} %get-tuple-element.95.cos_ref, f32[1024,128]{1,0:T(8,128)} %get-tuple-element.96.sin_ref), custom_call_target="tpu_custom_call" | custom-call | tf_op jit(solution)/shard_map/attend/pallas_call | solution.py:133
  292.3 1.7 convolution_convert_fusion.7
  293.9 6.9 convolution_convert_fusion.2
  300.9 44.2 %scatter_3.1 = f32[256,2176]{1,0:T(8,128)} custom-call(bf16[2,4,256,2048]{3,2,1,0:T(8,128)(2,1)} %bitcast.180, bf16[2,4,256,128]{3,2,1,0:T(8,128)(2,1)S(1)} %bitcast.162), custom_call_target="tpu_custom_call" | custom-call | bytes 100000000 | tf_op jit(solution)/shard_map/scatter_3/pallas_call | solution.py:602
  346.0 2.2 multiply_reduce_fusion.1
  349.4 42.9 %gather_4.1 = (bf16[2,4,256,2048]{3,2,1,0:T(8,128)(2,1)}, bf16[2,4,256,128]{3,2,1,0:T(8,128)(2,1)}) custom-call(bf16[256,2048]{1,0:T(8,128)(2,1)} %multiply_convert_fusion.4.refs_0_, bf16[256,128]{1,0:T(8,128)(2,1)} %copy-done.22), custom_call_target="tpu_custom_call" | custom-call | bytes 100000000 | tf_op jit(solution)/shard_map/gather_4/pallas_call | solution.py:440
  392.4 14.6 %fusion.64 = f32[2048,1024]{1,0:T(8,128)} fusion(bf16[2048,2048]{1,0:T(8,128)(2,1)} %bitcast.167, bf16[2048,1024]{1,0:T(8,128)(2,1)} %bitcast.249), kind=kOutput, calls=%fused_computation.163 | convolution fusion | flops 8589934592 | bytes 20971520 | tf_op jit(solution)/shard_map/dot_general | solution.py:22
  407.1 14.0 %all-gather.9.cloned.1.call-done = bf16[16,128,2304]{2,1,0:T(8,128)(2,1)} async-done(((bf16[4,128,2304]{2,1,0:T(8,128)(2,1)}), bf16[16,128,2304]{2,1,0:T(8,128)(2,1)}) %all-gather.9.cloned.1.call-update) | async-done | bytes 9437200 | tf_op jit(solution)/shard_map/all_gather | solution.py:921
  421.1 5.9 fusion.11
  428.1 13.0 %fusion.2 = f32[2048,1024]{1,0:T(8,128)} fusion(bf16[2048,2048]{1,0:T(8,128)(2,1)S(1)} %bitcast.176, bf16[2048,2304]{1,0:T(8,128)(2,1)} %bitcast.209), kind=kOutput, calls=%fused_computation.18 | convolution fusion | flops 8589934592 | bytes 20971520 | tf_op jit(solution)/shard_map/dot_general | solution.py:22
  441.1 13.4 %fusion.5 = f32[2048,1024]{1,0:T(8,128)} fusion(bf16[2048,2048]{1,0:T(8,128)(2,1)S(1)} %bitcast.177, bf16[2048,2304]{1,0:T(8,128)(2,1)} %bitcast.210), kind=kOutput, calls=%fused_computation.21 | convolution fusion | flops 8589934592 | bytes 20971520 | tf_op jit(solution)/shard_map/dot_general | solution.py:22
  454.6 2.2 convolution_add_fusion.2
  456.8 3.6 fusion.14
  460.5 5.5 convolution_add_fusion
  466.0 3.5 fusion.13
  469.4 13.6 %multiply_convert_fusion = (bf16[2048,1024]{1,0:T(8,128)(2,1)}, bf16[2048,1024]{1,0:T(8,128)(2,1)}, bf16[2048,1024]{1,0:T(8,128)(2,1)}) fusion(f32[2048,1024]{1,0:T(8,128)} %convolution_add_fusion, f32[2048,1024]{1,0:T(8,128)S(1)} %convolution_add_fusion.2, f32[2048,1024]{1,0:T(8,128)} %fusion.5, bf16[2048,128]{1,0:T(8,128)(2,1)S(1)} %fusion.13, ...), kind=kOutput, calls=%fused_computation.1 | convolution fusion | flops 572522496 | bytes 38535168 | tf_op jit(solution)/shard_map/dot_general | solution.py:22
  483.0 3.1 convolution_convert_fusion.8
  486.4 13.3 %convolution_convert_fusion.1 = bf16[2048,2048]{1,0:T(8,128)(2,1)} fusion(bf16[2048,1024]{1,0:T(8,128)(2,1)S(1)} %copy-done.12, bf16[2048,1024]{1,0:T(8,128)(2,1)} %bitcast.250), kind=kOutput, calls=%fused_computation.6 | convolution fusion | flops 8594128896 | bytes 16777216 | tf_op jit(solution)/shard_map/dot_general | solution.py:26
  501.9 1.4 convolution_convert_fusion.10
  503.4 14.0 %fusion = f32[2048,2048]{1,0:T(8,128)} fusion(bf16[2048,1024]{1,0:T(8,128)(2,1)S(1)} %copy-done.11, bf16[2048,2304]{1,0:T(8,128)(2,1)} %bitcast.213), kind=kOutput, calls=%fused_computation.16 | convolution fusion | flops 8589934592 | bytes 25165824 | tf_op jit(solution)/shard_map/dot_general | solution.py:26
  519.5 1.5 convolution_convert_fusion.9
  522.3 45.0 %scatter_5.1 = f32[256,2176]{1,0:T(8,128)} custom-call(bf16[2,4,256,2048]{3,2,1,0:T(8,128)(2,1)} %bitcast.190, bf16[2,4,256,128]{3,2,1,0:T(8,128)(2,1)S(1)} %bitcast.166), custom_call_target="tpu_custom_call" | custom-call | bytes 100000000 | tf_op jit(solution)/shard_map/scatter_5/pallas_call | solution.py:602
  568.2 3.2 multiply_convert_fusion.3.refs_3_
  571.4 15.4 %add_convert_fusion = bf16[2048,2048]{1,0:T(8,128)(2,1)} fusion(f32[2048,2048]{1,0:T(8,128)} %fusion, bf16[2048,1024]{1,0:T(8,128)(2,1)S(1)} %copy-done.10, bf16[2048,2304]{1,0:T(8,128)(2,1)} %bitcast.215), kind=kOutput, calls=%fused_computation | convolution fusion | flops 8598323200 | bytes 33554432 | tf_op jit(solution)/shard_map/dot_general | solution.py:26
  586.8 59.1 %scatter_7.1 = (f32[256,2304]{1,0:T(8,128)}, bf16[2,256,2048]{2,1,0:T(8,128)(2,1)}) custom-call(bf16[2,4,256,2048]{3,2,1,0:T(8,128)(2,1)} %bitcast.186, bf16[2,4,256,128]{3,2,1,0:T(8,128)(2,1)S(1)} %bitcast.164, bf16[2,4,256,128]{3,2,1,0:T(8,128)(2,1)S(1)} %bitcast.165, bf16[256,2048]{1,0:T(8,128)(2,1)} %multiply_convert_fusion.3.refs_3_), custom_call_target="tpu_custom_call" | custom-call | bytes 100000000 | tf_op jit(solution)/shard_map/scatter_7/pallas_call | solution.py:602
  647.8 1.5 fusion.41
  649.3 1.9 multiply_reduce_fusion
  651.3 2.2 fusion.59
  653.5 49.2 %gather_8.1 = (bf16[2,4,256,2048]{3,2,1,0:T(8,128)(2,1)}, bf16[2,4,256,384]{3,2,1,0:T(8,128)(2,1)}) custom-call(bf16[256,2048]{1,0:T(8,128)(2,1)} %get-tuple-element.54.refs_0_, bf16[256,384]{1,0:T(8,128)(2,1)} %pad_maximum_fusion.4.refs_1_), custom_call_target="tpu_custom_call" | custom-call | bytes 100000000 | tf_op jit(solution)/shard_map/gather_8/pallas_call | solution.py:440
  702.7 6.2 fusion.27
  710.1 2.4 fusion.15
  712.5 2.2 fusion.10.g_ref
  714.7 16.1 %attend_back.1 = bf16[2048,512]{1,0:T(8,128)(2,1)} custom-call(s32[2]{0:T(128)} %get-tuple-element.83.lengths, bf16[2048,512]{1,0:T(8,128)(2,1)} %get-tuple-element.43.low_ref, f32[2048,128]{1,0:T(8,128)} %get-tuple-element.44.lse_ref, bf16[2048,256]{1,0:T(8,128)(2,1)} %fusion.10.g_ref, f32[1024,128]{1,0:T(8,128)} %get-tuple-element.95.cos_ref, ...), custom_call_target="tpu_custom_call" | custom-call | tf_op jit(solution)/shard_map/attend_back/pallas_call | solution.py:151
  730.9 8.5 convolution_convert_fusion
  739.4 1.7 convolution_convert_fusion.3
  744.1 62.6 %scatter_9.1 = (f32[256,2176]{1,0:T(8,128)}, f32[4,8,3072]{2,1,0:T(8,128)S(1)}) custom-call(bf16[2,4,256,2048]{3,2,1,0:T(8,128)(2,1)} %bitcast.187, bf16[2,4,256,128]{3,2,1,0:T(8,128)(2,1)S(1)} %bitcast.163, bf16[4,4,8,3072]{3,2,1,0:T(8,128)(2,1)S(1)} %bitcast.161), custom_call_target="tpu_custom_call" | custom-call | bytes 100000000 | tf_op jit(solution)/shard_map/scatter_9/pallas_call | solution.py:602
  806.7 1.5 multiply_convert_fusion.6.refs_0_
  808.2 10.5 %gather_10.1 = bf16[2,4,256,128]{3,2,1,0:T(8,128)(2,1)} custom-call(bf16[256,128]{1,0:T(8,128)(2,1)} %multiply_convert_fusion.6.refs_0_), custom_call_target="tpu_custom_call" | custom-call | bytes 100000000 | tf_op jit(solution)/shard_map/gather_10/pallas_call | solution.py:440
  818.7 3.6 fusion.19
  822.4 4.2 entry_grads.2
  826.6 6.4 entry_grads.3
  833.0 2.0 pad_maximum_fusion.1.rows_ref
  835.7 3.7 fusion.22.depart_ref
  839.4 56.5 %collect_11.1 = (f32[4,8,768]{2,1,0:T(8,128)}, f32[128,640]{1,0:T(8,128)}, bf16[2,256,2048]{2,1,0:T(8,128)(2,1)}) custom-call(bf16[4,4,8,768]{3,2,1,0:T(8,128)(2,1)} %bitcast.228, bf16[4,128,640]{2,1,0:T(8,128)(2,1)} %pad_maximum_fusion.1.rows_ref, bf16[256,2048]{1,0:T(8,128)(2,1)} %fusion.22.depart_ref), custom_call_target="tpu_custom_call" | custom-call | bytes 60000000 | tf_op jit(solution)/shard_map/collect_11/pallas_call | solution.py:760
  895.8 1.4 fusion.62
  897.2 1.3 slice_bitcast_fusion
  898.6 3.2 reshape.356
  901.8 2.4 copy.62
  904.2 4.5 reshape.357
  910.2 3.2 reshape.345
  913.4 2.4 copy.61
  915.8 4.5 reshape.346
  (180 shorter events, 38.9 us)
Async XLA Ops:
  7.2 255.4 %all-gather.11.cloned.1.call-start = ((), (), s32[]{:S(2)}) async-start(), calls=%async_computation.2 | async-start | bytes 4587520 | tf_op jit(solution)/shard_map/all_gather | solution.py:921
  12.3 5.5 copy-start.30
  12.3 5.5 copy-start.31
  12.4 6.3 copy-start.32
  18.7 1.5 copy-start.25
  78.7 313.7 %all-gather.7.cloned.1.call-start = ((), (), s32[]{:S(2)}) async-start(), calls=%async_computation | async-start | bytes 5242880 | tf_op jit(solution)/shard_map/all_gather | solution.py:921
  81.9 84.7 %copy-start.46 = (s32[2]{0:T(128)S(1)}, s32[2]{0:T(128)}, u32[]{:S(2)}) copy-start(s32[2]{0:T(128)} %param.28) | copy-start | bytes 28
  81.9 84.8 %copy-start.47 = (s32[2]{0:T(128)S(1)}, s32[2]{0:T(128)}, u32[]{:S(2)}) copy-start(s32[2]{0:T(128)} %param.27) | copy-start | bytes 28
  81.9 85.6 %copy-start.43 = (bf16[2048]{0:T(1024)(128)(2,1)S(1)}, bf16[2048]{0:T(1024)(128)(2,1)}, u32[]{:S(2)}) copy-start(bf16[2048]{0:T(1024)(128)(2,1)} %param.29) | copy-start | bytes 12292
  81.9 85.6 %copy-start.1 = (bf16[256,2048]{1,0:T(8,128)(2,1)S(1)}, bf16[256,2048]{1,0:T(8,128)(2,1)}, u32[]{:S(2)}) copy-start(bf16[256,2048]{1,0:T(8,128)(2,1)} %get-tuple-element.38) | copy-start | bytes 3145732
  165.9 255.1 %all-gather.9.cloned.1.call-start = ((), (), s32[]{:S(2)}) async-start(), calls=%async_computation.1 | async-start | bytes 11796480 | tf_op jit(solution)/shard_map/all_gather | solution.py:921
  166.7 51.2 %collective-permute-start = (s32[2,2]{1,0:T(2,128)S(1)}, s32[2,2]{1,0:T(2,128)S(1)}, u32[]{:S(2)}, u32[]{:S(2)}) collective-permute-start(s32[2,2]{1,0:T(2,128)S(1)} %pad_add_fusion), channel_id=1, source_target_pairs={{0,0},{2,8},{4,16},{6,24},{8,2},{10,10},{12,18},{14,26},{16,4},{18... | collective-permute-start | bytes 56 | tf_op jit(solution)/shard_map/ppermute | solution.py:931
  167.5 0.9 copy-start.26
  167.9 0.6 copy-start.39
  168.4 0.6 copy-start.35
  170.3 44.3 %copy-start.44 = (bf16[2048]{0:T(1024)(128)(2,1)S(1)}, bf16[2048]{0:T(1024)(128)(2,1)}, u32[]{:S(2)}) copy-start(bf16[2048]{0:T(1024)(128)(2,1)} %param.30) | copy-start | bytes 12292
  214.6 5.1 copy-start.13
  214.6 133.6 %copy-start.28 = (f32[4,4,128]{2,1,0:T(4,128)}, f32[4,4,128]{2,1,0:T(4,128)S(1)}, u32[]{:S(2)}) copy-start(f32[4,4,128]{2,1,0:T(4,128)S(1)} %copy.60) | copy-start | bytes 24580
  219.7 42.3 %copy-start.33 = (f32[256]{0:T(256)}, f32[256]{0:T(256)S(1)}, u32[]{:S(2)}) copy-start(f32[256]{0:T(256)S(1)} %compare_convert_fusion.1) | copy-start | bytes 3076
  262.6 11.0 %slice-start = ((s8[8388608]{0:T(1024)(128)(4,1)}), s8[4194304]{0:T(1024)(128)(4,1)S(1)}, s32[]{:S(2)}) async-start(s8[8388608]{0:T(1024)(128)(4,1)} %bitcast.172), calls=%async_computation.3 | async-start | bytes 8388608
  263.9 9.6 %collective-permute-start.1 = (bf16[2048,128]{1,0:T(8,128)(2,1)S(1)}, bf16[2048,128]{1,0:T(8,128)(2,1)S(1)}, u32[]{:S(2)}, u32[]{:S(2)}) collective-permute-start(bf16[2048,128]{1,0:T(8,128)(2,1)S(1)} %slice.179), channel_id=1, source_target_pairs={{0,1},{1,0},{2,3},{3,2},{4,5},{5,4},{6,7},{7,6},{8,9},{9,8},{10,11... | collective-permute-start | bytes 1572872 | tf_op jit(solution)/shard_map/ppermute | solution.py:924
  264.4 9.2 slice-start.1
  264.4 9.2 copy-start.15
  273.6 72.3 %copy-start.6 = (bf16[2048,128]{1,0:T(8,128)(2,1)}, bf16[2048,128]{1,0:T(8,128)(2,1)S(1)}, u32[]{:S(2)}) copy-start(bf16[2048,128]{1,0:T(8,128)(2,1)S(1)} %collective-permute-done.1) | copy-start | bytes 1572868
  276.0 3.8 copy-start.8
  346.0 3.5 copy-start.22
  348.2 58.9 %copy-start.41 = (f32[256]{0:T(256)}, f32[256]{0:T(256)S(1)}, u32[]{:S(2)}) copy-start(f32[256]{0:T(256)S(1)} %get-tuple-element.85) | copy-start | bytes 3076
  348.2 58.9 %copy-start.37 = (f32[256]{0:T(256)}, f32[256]{0:T(256)S(1)}, u32[]{:S(2)}) copy-start(f32[256]{0:T(256)S(1)} %add_rsqrt_fusion) | copy-start | bytes 3076
  421.1 7.0 copy-start
  428.1 26.5 %slice-start.4 = ((s8[8388608]{0:T(1024)(128)(4,1)}), s8[4194304]{0:T(1024)(128)(4,1)S(1)}, s32[]{:S(2)}) async-start(s8[8388608]{0:T(1024)(128)(4,1)} %bitcast.188), calls=%async_computation.7 | async-start | bytes 8388608
  441.1 13.5 %slice-start.5 = ((s8[8388608]{0:T(1024)(128)(4,1)}), s8[4194304]{0:T(1024)(128)(4,1)S(1)}, s32[]{:S(2)}) async-start(s8[8388608]{0:T(1024)(128)(4,1)} %bitcast.188), calls=%async_computation.8 | async-start | bytes 8388608
  454.5 2.3 collective-permute-start.2
  456.8 3.6 copy-start.5
  483.0 3.4 copy-start.12
  486.4 13.3 %copy-start.21 = (bf16[4,4,8,3840]{3,2,1,0:T(8,128)(2,1)S(1)}, bf16[4,4,8,3840]{3,2,1,0:T(8,128)(2,1)}, u32[]{:S(2)}) copy-start(bf16[4,4,8,3840]{3,2,1,0:T(8,128)(2,1)} %get-tuple-element.37) | copy-start | bytes 2949124
  499.7 2.2 copy-start.11
  517.3 2.2 copy-start.10
  522.3 45.9 %copy-start.34 = (f32[256]{0:T(256)S(1)}, f32[256]{0:T(256)}, u32[]{:S(2)}) copy-start(f32[256]{0:T(256)} %copy-done.33) | copy-start | bytes 3076
  586.8 59.1 %copy-start.45 = (f32[1,256]{1,0:T(1,128)S(1)}, f32[1,256]{1,0:T(1,128)}, u32[]{:S(2)}) copy-start(f32[1,256]{1,0:T(1,128)} %pad_maximum_fusion.6) | copy-start | bytes 3076
  586.8 62.5 %copy-start.29 = (f32[4,4,128]{2,1,0:T(4,128)S(1)}, f32[4,4,128]{2,1,0:T(4,128)}, u32[]{:S(2)}) copy-start(f32[4,4,128]{2,1,0:T(4,128)} %copy-done.28) | copy-start | bytes 24580
  645.9 3.3 copy-start.17
  649.3 2.0 copy-start.42
  649.3 2.0 copy-start.14
  649.3 2.0 copy-start.38
  702.7 6.3 slice-start.2
  702.7 6.3 slice-start.3
  702.7 6.3 copy-start.7
  702.7 7.3 copy-start.16
  730.9 8.6 copy-start.3
  730.9 10.3 %copy-start.18 = (bf16[2,4,256,384]{3,2,1,0:T(8,128)(2,1)S(1)}, bf16[2,4,256,384]{3,2,1,0:T(8,128)(2,1)}, u32[]{:S(2)}) copy-start(bf16[2,4,256,384]{3,2,1,0:T(8,128)(2,1)} %get-tuple-element.48) | copy-start | bytes 4718596
  739.4 3.7 copy-start.9
  739.4 4.2 copy-start.4
  741.2 2.8 copy-start.19
  741.2 2.8 copy-start.20
  744.1 74.6 %copy-start.2 = (bf16[256,2048]{1,0:T(8,128)(2,1)S(1)}, bf16[256,2048]{1,0:T(8,128)(2,1)}, u32[]{:S(2)}) copy-start(bf16[256,2048]{1,0:T(8,128)(2,1)} %get-tuple-element.38) | copy-start | bytes 3145732
  744.1 74.6 %copy-start.27 = (f32[4,4,128]{2,1,0:T(4,128)S(1)}, f32[4,4,128]{2,1,0:T(4,128)}, u32[]{:S(2)}) copy-start(f32[4,4,128]{2,1,0:T(4,128)} %copy-done.26) | copy-start | bytes 24580
  806.7 15.7 %copy-start.40 = (f32[256]{0:T(256)S(1)}, f32[256]{0:T(256)}, u32[]{:S(2)}) copy-start(f32[256]{0:T(256)} %copy-done.39) | copy-start | bytes 3076
  826.6 6.4 copy-start.23
  826.6 9.1 copy-start.36
  901.8 6.9 copy-start.24
Sparse Core Ops, SparseCore 0:
  78.8 94.2 all-gather.10
  174.7 79.4 all-gather.6
  255.8 165.2 all-gather.8
